TPU v7x, 32 devices: a 4x4x1 block of a 4x4x8 slice. The times are simulated.
32 devices in a mesh: dp: 1 (over z), cy: 4 (over y), cx: 4 (over x), core: 2 (over core).
Axes of the slice: x: 4, y: 4, z: 1, core: 2. Of those that a mesh axis runs over, the one named last changes fastest.
The devices are a block of a 4x4x8 slice.
Arguments:
- x_in: bfloat16 [1, 3072, 2048], P('dp', ('cy', 'cx', 'core'))
- w_qkv: bfloat16 [2048, 48, 64], replicated
- w_out: bfloat16 [32, 64, 2048], replicated
Outputs:
- output: bfloat16 [1, 3072, 2048], P('dp', ('cy', 'cx', 'core'))
All inputs are finite; a program needn't handle non-finite values.
Results may differ from a plain program's by a relative error of at most 0.00796281.
Values are sent between devices in bfloat16 or wider.
A program may use at most 768 MiB of HBM per device.

v0:
```python
import jax
import jax.numpy as jnp
from jax import lax
from jax.sharding import PartitionSpec as P


def solution(mesh):
    cy_size = mesh.shape["cy"]
    head_split = mesh.shape["cx"] * mesh.shape["core"]
    seq_spec = P("dp", ("cy", "cx", "core"))

    def local_layer(x_loc, w_qkv, w_out):
        num_heads = w_out.shape[0]
        head_dim = w_out.shape[1]
        num_kv = (w_qkv.shape[1] - num_heads) // 2
        num_tokens = x_loc.shape[1]
        kv_slots = max(num_kv, head_split)
        repeat_kv = kv_slots // num_kv
        q_local = num_heads // head_split
        kv_local = kv_slots // head_split
        group_size = q_local // kv_local
        qkv_rows = jnp.einsum("sc,chd->shd", x_loc[0], w_qkv, preferred_element_type=jnp.float32).astype(jnp.bfloat16)
        q_part = qkv_rows[:, :num_heads].reshape(num_tokens, head_split, q_local, head_dim)
        k_part = jnp.repeat(qkv_rows[:, num_heads:num_heads + num_kv], repeat_kv, axis=1).reshape(num_tokens, head_split, kv_local, head_dim)
        v_part = jnp.repeat(qkv_rows[:, num_heads + num_kv:], repeat_kv, axis=1).reshape(num_tokens, head_split, kv_local, head_dim)
        packed = jnp.concatenate([q_part, k_part, v_part], axis=2)
        packed = lax.all_to_all(packed, "cx", 1, 0, tiled=True)
        packed = lax.all_to_all(packed, "core", 1, 0, tiled=True)
        seq_len = packed.shape[0]
        queries = packed[:, 0, :q_local].reshape(seq_len, kv_local, group_size, head_dim)
        kv_all = lax.all_gather(packed[:, 0, q_local:], "cy")
        logit_scale = head_dim ** -0.5
        run_max = jnp.full((kv_local, group_size, seq_len), -jnp.inf, jnp.float32)
        run_sum = jnp.zeros((kv_local, group_size, seq_len), jnp.float32)
        accumulator = jnp.zeros((kv_local, group_size, seq_len, head_dim), jnp.float32)
        for block_idx in range(cy_size):
            k_block = kv_all[block_idx, :, :kv_local]
            v_block = kv_all[block_idx, :, kv_local:]
            scores = jnp.einsum("qkgd,skd->kgqs", queries, k_block, preferred_element_type=jnp.float32) * logit_scale
            new_max = jnp.maximum(run_max, scores.max(axis=-1))
            rescale = jnp.exp(run_max - new_max)
            weights = jnp.exp(scores - new_max[..., None])
            run_sum = run_sum * rescale + weights.sum(axis=-1)
            accumulator = accumulator * rescale[..., None] + jnp.einsum("kgqs,skd->kgqd", weights.astype(jnp.bfloat16), v_block, preferred_element_type=jnp.float32)
            run_max = new_max
        attn_out = (accumulator / run_sum[..., None]).astype(jnp.bfloat16)
        attn_out = jnp.transpose(attn_out, (2, 0, 1, 3)).reshape(seq_len, q_local, head_dim)
        attn_out = lax.all_to_all(attn_out, "core", 0, 1, tiled=True)
        attn_out = lax.all_to_all(attn_out, "cx", 0, 1, tiled=True)
        y_local = jnp.einsum("shd,hdc->sc", attn_out, w_out, preferred_element_type=jnp.float32)
        return y_local.astype(jnp.bfloat16)[None]

    return jax.shard_map(local_layer, mesh=mesh, in_specs=(seq_spec, P(), P()), out_specs=seq_spec, check_vma=False)
```

profile of v0, /device:TPU:97, one launch (start us, length us, event | category | flops | bytes accessed | tf_op | source)
XLA Modules:
  0.0 93.0 jit_solution(9718071272269123768)
XLA Ops:
  0.0 0.0 copy-start
  0.0 1.0 %copy-done = bf16[1,96,2048]{2,1,0:T(8,128)(2,1)S(1)} copy-done((bf16[1,96,2048]{2,1,0:T(8,128)(2,1)S(1)}, bf16[1,96,2048]{2,1,0:T(8,128)(2,1)}, u32[]{:S(2)}) %copy-start) | copy-done | bytes 393240
  1.0 6.5 %fusion.56 = f32[96,3072]{0,1:S(1)} fusion(bf16[2048,3072]{0,1:T(8,128)(2,1)} %bitcast.222, bf16[1,96,2048]{2,1,0:T(8,128)(2,1)S(1)} %copy-done), kind=kOutput, calls=%fused_computation.44 | convolution fusion | flops 1207959552 | bytes 14155776
  7.5 0.1 convert_element_type.24
  7.7 0.2 pad_maximum_fusion
  7.9 16.3 %all_to_all.72 = bf16[96,8,6,64]{0,3,2,1:T(8,128)(2,1)S(1)} all-to-all(bf16[96,8,6,64]{0,3,2,1:T(8,128)(2,1)S(1)} %pad_maximum_fusion), channel_id=1, replica_groups=mesh['dp'=1,'cy'=4,'cx'=4,'core'=2] {'cx'}, dimensions={1} | all-to-all | bytes 1179648 | tf_op jit(solution)/shard_map/all_to_all | solution.py:27
  24.2 0.6 copy.118
  24.8 0.5 all_to_all.55
  25.3 5.7 %all_to_all.73 = bf16[384,2,6,64]{0,3,2,1:T(8,128)(2,1)S(1)} all-to-all(bf16[384,2,6,64]{0,3,2,1:T(8,128)(2,1)S(1)} %all_to_all.55), channel_id=1, replica_groups=mesh['dp'=1,'cy'=4,'cx'=4,'core'=2] {'core'}, dimensions={1} | all-to-all | bytes 1179648 | tf_op jit(solution)/shard_map/all_to_all | solution.py:28
  31.0 0.1 copy.92
  31.1 14.0 %all-gather = bf16[3072,1,2,64]{0,3,2,1:T(8,128)(2,1)S(1)} all-gather(bf16[768,1,2,64]{0,3,2,1:T(8,128)(2,1)S(1)} %slice.55), channel_id=2, replica_groups=mesh['dp'=1,'cy'=4,'cx'=4,'core'=2] {'cy'}, dimensions={0}, use_global_device_ids=true | all-gather | bytes 983040 | tf_op jit(solution)/shard_map/all_gather | solution.py:31
  45.1 0.6 reshape.256
  45.7 1.1 %fusion.67 = (bf16[1,768,1,64]{1,0,3,2:T(2,128)(2,1)S(1)}, bf16[1,768,1,64]{1,0,3,2:T(2,128)(2,1)S(1)}, bf16[1,768,1,64]{1,0,3,2:T(2,128)(2,1)S(1)}, bf16[1,768,...) fusion(bf16[4,768,2,64]{1,0,3,2:T(4,128)(2,1)S(1)} %reshape.256), kind=kLoop, calls=%fused_computation.70 | loop fusion | bytes 1572864 | tf_op jit(solution)/shard_map/slice | solution.py:38
  46.9 1.4 %bitcast_reduce_fusion = (f32[4,768]{1,0:T(4,128)S(1)}, f32[768,768,4]{1,0,2:T(8,128)S(1)}) fusion(bf16[768,1,6,64]{0,3,2,1:T(8,128)(2,1)S(1)} %bitcast.224, bf16[1,768,1,64]{1,0,3,2:T(2,128)(2,1)S(1)} %get-tuple-element.13), kind=kOutput, calls=%fused_computation.1 | convolution fusion | flops 306705408 | bytes 10039296 | tf_op jit(solution)/shard_map/qkgd,skd->kgqs/dot_general | solution.py:39
  48.3 1.4 %bitcast_reduce_fusion.1 = (f32[4,768]{1,0:T(4,128)S(1)}, f32[768,768,4]{1,0,2:T(8,128)S(1)}) fusion(bf16[768,1,6,64]{0,3,2,1:T(8,128)(2,1)S(1)} %bitcast.225, bf16[1,768,1,64]{1,0,3,2:T(2,128)(2,1)S(1)} %get-tuple-element.15), kind=kOutput, calls=%fused_computation.4 | convolution fusion | flops 306705408 | bytes 10039296 | tf_op jit(solution)/shard_map/qkgd,skd->kgqs/dot_general | solution.py:39
  49.7 1.4 %bitcast_reduce_fusion.2 = (f32[4,768]{1,0:T(4,128)S(1)}, f32[768,768,4]{1,0,2:T(8,128)S(1)}) fusion(bf16[768,1,6,64]{0,3,2,1:T(8,128)(2,1)S(1)} %bitcast.226, bf16[1,768,1,64]{1,0,3,2:T(2,128)(2,1)S(1)} %get-tuple-element.17), kind=kOutput, calls=%fused_computation.7 | convolution fusion | flops 306705408 | bytes 10039296 | tf_op jit(solution)/shard_map/qkgd,skd->kgqs/dot_general | solution.py:39
  51.1 1.4 %bitcast_reduce_fusion.3 = (f32[4,768]{1,0:T(4,128)S(1)}, f32[768,768,4]{1,0,2:T(8,128)S(1)}) fusion(bf16[768,1,6,64]{0,3,2,1:T(8,128)(2,1)S(1)} %bitcast.227, bf16[1,768,1,64]{1,0,3,2:T(2,128)(2,1)S(1)} %get-tuple-element.19), kind=kOutput, calls=%fused_computation.10 | convolution fusion | flops 306705408 | bytes 10039296 | tf_op jit(solution)/shard_map/qkgd,skd->kgqs/dot_general | solution.py:39
  52.6 3.3 %fusion.4 = (f32[4,768]{1,0:T(4,128)S(1)}, f32[4,768]{1,0:T(4,128)S(1)}) fusion(f32[768,768,4]{1,0,2:T(8,128)S(1)} %get-tuple-element.24, f32[4,768]{1,0:T(4,128)S(1)} %get-tuple-element.23, f32[4,768]{1,0:T(4,128)S(1)} %get-tuple-element.9, f32[768,768,4]{1,0,2:T(8,128)S(1)} %get-tuple-element.26), kind=kLoop, calls=%fused_computation.12 | loop fusion | flops 14149632 | bytes 18923520 | tf_op jit(solution)/shard_map/reduce_sum | solution.py:43
  55.9 3.1 %fusion.6 = (f32[4,768]{1,0:T(4,128)S(1)}, f32[4,768]{1,0:T(4,128)S(1)}) fusion(f32[768,768,4]{1,0,2:T(8,128)S(1)} %get-tuple-element.30, f32[4,768]{1,0:T(4,128)S(1)} %get-tuple-element.11, f32[4,768]{1,0:T(4,128)S(1)} %get-tuple-element.10, f32[768,768,4]{1,0,2:T(8,128)S(1)} %get-tuple-element.28), kind=kLoop, calls=%fused_computation.14 | loop fusion | flops 14149632 | bytes 18923520 | tf_op jit(solution)/shard_map/reduce_sum | solution.py:43
  59.1 1.7 %fusion.38 = f32[4,768,64]{1,2,0:T(8,128)S(1)} fusion(f32[768,768,4]{1,0,2:T(8,128)S(1)} %get-tuple-element.24, f32[4,768]{1,0:T(4,128)S(1)} %get-tuple-element.23, f32[4,768]{1,0:T(4,128)S(1)} %get-tuple-element.8, f32[4,768]{1,0:T(4,128)S(1)} %get-tuple-element.22, bf16[1,768,1,64]{1,0,3,2:T(2,128)(2,1)S(1)} %get-tuple-element.18), kind=kOutput, calls=%fused_computation.35 | convolution fusion | flops 309460992 | bytes 10358784 | tf_op jit(solution)/shard_map/kgqs,skd->kgqd/dot_general | solution.py:44
  60.9 1.8 %fusion.41 = f32[4,768,64]{1,2,0:T(8,128)S(1)} fusion(f32[4,768,64]{1,2,0:T(8,128)S(1)} %fusion.38, f32[768,768,4]{1,0,2:T(8,128)S(1)} %get-tuple-element.30, f32[4,768]{1,0:T(4,128)S(1)} %get-tuple-element.11, f32[4,768]{1,0:T(4,128)S(1)} %get-tuple-element.7, bf16[1,768,1,64]{1,0,3,2:T(2,128)(2,1)S(1)} %get-tuple-element.16), kind=kOutput, calls=%fused_computation.36 | convolution fusion | flops 309460992 | bytes 11132928 | tf_op jit(solution)/shard_map/kgqs,skd->kgqd/dot_general | solution.py:44
  62.6 1.8 %fusion.44 = f32[4,768,64]{1,2,0:T(8,128)S(1)} fusion(f32[4,768,64]{1,2,0:T(8,128)S(1)} %fusion.41, f32[768,768,4]{1,0,2:T(8,128)S(1)} %get-tuple-element.28, f32[4,768]{1,0:T(4,128)S(1)} %get-tuple-element.10, f32[4,768]{1,0:T(4,128)S(1)} %get-tuple-element.6, bf16[1,768,1,64]{1,0,3,2:T(2,128)(2,1)S(1)} %get-tuple-element.14), kind=kOutput, calls=%fused_computation.37 | convolution fusion | flops 309460992 | bytes 11132928 | tf_op jit(solution)/shard_map/kgqs,skd->kgqd/dot_general | solution.py:44
  64.4 1.8 %fusion.53 = bf16[768,4,64]{0,2,1:T(8,128)(2,1)S(1)} fusion(f32[4,768,64]{1,2,0:T(8,128)S(1)} %fusion.44, f32[768,768,4]{1,0,2:T(8,128)S(1)} %get-tuple-element.26, f32[4,768]{1,0:T(4,128)S(1)} %get-tuple-element.9, f32[4,768]{1,0:T(4,128)S(1)} %get-tuple-element.5, bf16[1,768,1,64]{1,0,3,2:T(2,128)(2,1)S(1)} %get-tuple-element.12), kind=kOutput, calls=%fused_computation.40 | convolution fusion | flops 309657600 | bytes 10739712 | tf_op jit(solution)/shard_map/kgqs,skd->kgqd/dot_general | solution.py:44
  66.1 0.6 copy.72
  66.7 0.7 reshape.268
  67.4 5.7 %all_to_all.74 = bf16[2,2,49152]{2,1,0:T(2,128)(2,1)S(1)} all-to-all(bf16[2,2,49152]{2,1,0:T(2,128)(2,1)S(1)} %reshape.268), channel_id=1, replica_groups=mesh['dp'=1,'cy'=4,'cx'=4,'core'=2] {'core'}, dimensions={0} | all-to-all | bytes 786432 | tf_op jit(solution)/shard_map/all_to_all | solution.py:48
  73.2 0.6 reshape.269
  73.8 0.8 copy.82
  74.5 0.1 copy.74
  74.6 0.5 copy.75
  75.1 0.6 reshape.270
  75.7 0.0 copy-start.1
  75.7 10.4 %all_to_all.75 = bf16[4,2,24576]{2,1,0:T(2,128)(2,1)S(1)} all-to-all(bf16[4,2,24576]{2,1,0:T(2,128)(2,1)S(1)} %reshape.270), channel_id=1, replica_groups=mesh['dp'=1,'cy'=4,'cx'=4,'core'=2] {'cx'}, dimensions={0} | all-to-all | bytes 786432 | tf_op jit(solution)/shard_map/all_to_all | solution.py:49
  86.0 0.5 reshape.271
  86.5 0.6 copy.83
  87.2 0.1 copy.77
  87.3 5.7 %fusion.25 = bf16[1,96,2048]{2,1,0:T(8,128)(2,1)} fusion(bf16[96,32,64]{0,2,1:T(8,128)(2,1)S(1)} %bitcast.229, bf16[32,64,2048]{2,1,0:T(8,128)(2,1)} %param.5), kind=kOutput, calls=%fused_computation.30 | convolution fusion | flops 805502976 | bytes 9175040 | tf_op jit(solution)/shard_map/shd,hdc->sc/dot_general | solution.py:50
  93.0 0.0 copy-done.1
  (5 shorter events, 0.1 us)
Async XLA Ops:
  0.0 1.0 %copy-start = (bf16[1,96,2048]{2,1,0:T(8,128)(2,1)S(1)}, bf16[1,96,2048]{2,1,0:T(8,128)(2,1)}, u32[]{:S(2)}) copy-start(bf16[1,96,2048]{2,1,0:T(8,128)(2,1)} %param.3) | copy-start | bytes 1179652
  75.7 17.3 %copy-start.1 = (bf16[1,96,2048]{2,1,0:T(8,128)(2,1)S(1)}, bf16[1,96,2048]{2,1,0:T(8,128)(2,1)}, u32[]{:S(2)}) copy-start(bf16[1,96,2048]{2,1,0:T(8,128)(2,1)} %param.3) | copy-start | bytes 1179652
where the time goes:
time: 93.4 us; the launch traced here: 93 us
  blocking collectives  52.1 us (56%)
  matrix products  24.8 us (27%)
  local copies, waits for them, and re-layouts  8.99 us (10%)
  other arithmetic  6.83 us (7%)
    all_to_all x1, blocking collectives, local_layer(): packed = lax.all_to_all(packed, 'cx', 1, 0, tiled=True)  16.3 us
    all_gather x1, blocking collectives, local_layer(): kv_all = lax.all_gather(packed[:, 0, q_local:], 'cy')  14 us
    all_to_all x1, blocking collectives, local_layer(): attn_out = lax.all_to_all(attn_out, 'cx', 0, 1, tiled=True)  10.4 us
    dot_general x4, matrix products, local_layer(): jnp.einsum('kgqs,skd->kgqd', weights.astype(jnp.bfloat16), v_block, prefe...  7.02 us
    reduce_sum x2, other arithmetic, local_layer(): run_sum = run_sum * rescale + weights.sum(axis=-1)  6.48 us
    unnamed x1, matrix products  6.46 us
    all_to_all x1, blocking collectives, local_layer(): attn_out = lax.all_to_all(attn_out, 'core', 0, 1, tiled=True)  5.72 us
    all_to_all x1, blocking collectives, local_layer(): packed = lax.all_to_all(packed, 'core', 1, 0, tiled=True)  5.71 us

commit v1 on v0

v1 whole, which is shorter than its diff:
```python
import functools
import math

import jax
import jax.numpy as jnp
from jax import lax
from jax.experimental import pallas as pl
from jax.experimental.pallas import tpu as pltpu
from jax.sharding import PartitionSpec as P

MESH = pl.DeviceIdType.MESH
LANES = 128
TILE = 256
NT = (((1,), (1,)), ((), ()))

ORDER = (
    (0, 0),
    (1, 0), (3, 0), (0, 1), (0, 3),
    (2, 0), (0, 2), (1, 1), (3, 3), (1, 3), (3, 1),
    (2, 1), (1, 2), (2, 3), (3, 2),
    (2, 2),
)


def kernel(dims, x_hbm, wqkv_hbm, wout_hbm, y_ref,
           x_ext, w_kv, w_q, w_o, kv_buf, q_t, acc, stat, o_buf, o_recv,
           load_sem, x_sem, kv_send, kv_recv, o_sem):
    nx, ny, heads, kv_heads, head_dim = dims
    chip_tokens = o_buf.shape[0]
    dev_tokens = chip_tokens // 2
    kv_local = kv_heads // 2
    group = heads // kv_heads
    q_rows = group * head_dim
    feat = kv_local * q_rows
    rows = q_t.shape[2]
    main = LANES
    tail = chip_tokens - main
    cx, cy, core = lax.axis_index("cx"), lax.axis_index("cy"), lax.axis_index("core")
    other = 1 - core
    own_rows = pl.ds(pl.multiple_of(core * dev_tokens, 32), dev_tokens)
    other_rows = pl.ds(pl.multiple_of(other * dev_tokens, 32), dev_tokens)

    x_load = pltpu.make_async_copy(x_hbm, x_ext.at[own_rows], load_sem.at[0])
    x_load.start()
    kv_loads = []
    for h in range(kv_local):
        head = core * kv_local + h
        for part in range(2):
            src = pl.multiple_of((heads + part * kv_heads + head) * head_dim, head_dim)
            copy = pltpu.make_async_copy(
                wqkv_hbm.at[pl.ds(src, head_dim)],
                w_kv.at[pl.ds(h * 2 * head_dim + part * head_dim, head_dim)],
                load_sem.at[1 + 2 * h + part])
            copy.start()
            kv_loads.append(copy)
    q_load = pltpu.make_async_copy(
        wqkv_hbm.at[pl.ds(pl.multiple_of(core * feat, feat), feat)], w_q, load_sem.at[1 + 2 * kv_local])
    q_load.start()

    def chip(dx, dy):
        return {"cx": lax.rem(cx + dx, nx), "cy": lax.rem(cy + dy, ny)}

    barrier = pltpu.get_barrier_semaphore()
    for target in ({"core": other}, chip(1, 0), chip(nx - 1, 0), chip(0, 1), chip(0, ny - 1)):
        pl.semaphore_signal(barrier, inc=1, device_id=target, device_id_type=MESH)
    pl.semaphore_wait(barrier, 5)

    x_load.wait()
    x_copy = pltpu.make_async_remote_copy(
        src_ref=x_ext.at[own_rows], dst_ref=x_ext.at[own_rows], send_sem=x_sem.at[0], recv_sem=x_sem.at[1],
        device_id={"core": other}, device_id_type=MESH)
    x_copy.start()
    q_t[:, head_dim:, :] = jnp.zeros((kv_local, LANES - head_dim, rows), jnp.bfloat16)
    x_copy.wait()
    x_ext[chip_tokens:chip_tokens + tail] = x_ext[main:chip_tokens]

    def send(slot, kind, half, target):
        width = kv_local // 2
        first = kind * width
        if half is not None:
            width //= 2
            first = first + half * width
        ref = kv_buf.at[slot, pl.ds(first, width)]
        pltpu.make_async_remote_copy(
            src_ref=ref, dst_ref=ref, send_sem=kv_send, recv_sem=kv_recv.at[slot, kind],
            device_id=target, device_id_type=MESH).start()

    def slot_of(dx, dy):
        return lax.rem(cy + dy, ny) * nx + lax.rem(cx + dx, nx)

    mine = slot_of(0, 0)
    for kind in range(2):
        for copy in kv_loads[kind * kv_local:(kind + 1) * kv_local]:
            copy.wait()
        part = lax.dot_general(
            x_ext[:chip_tokens], w_kv[kind * TILE:(kind + 1) * TILE], NT, preferred_element_type=jnp.float32)
        for h in range(2):
            kv_buf[mine, kind * 2 + h] = part[:, h * LANES:(h + 1) * LANES].astype(jnp.bfloat16)
        for target in (chip(1, 0), chip(nx - 1, 0), chip(0, 1), chip(0, ny - 1)):
            send(mine, kind, None, target)

    o_load = pltpu.make_async_copy(wout_hbm, w_o, load_sem.at[2 + 2 * kv_local])
    o_load.start()

    q_load.wait()
    lane = lax.broadcasted_iota(jnp.int32, (head_dim, LANES), 1)
    for h in range(kv_local):
        res = lax.dot_general(
            w_q[h * q_rows:(h + 1) * q_rows], x_ext[...], NT, preferred_element_type=jnp.float32)
        for g in range(group):
            q_t[h, :head_dim, g * LANES:(g + 1) * LANES] = (
                res[g * head_dim:(g + 1) * head_dim, :main].astype(jnp.bfloat16))
        for pair in range(group // 2):
            lo = res[2 * pair * head_dim:(2 * pair + 1) * head_dim, main:]
            hi = res[(2 * pair + 1) * head_dim:(2 * pair + 2) * head_dim, main:]
            q_t[h, :head_dim, (group + pair) * LANES:(group + pair + 1) * LANES] = (
                jnp.where(lane < tail, lo, hi).astype(jnp.bfloat16))

    acc[...] = jnp.zeros_like(acc)
    stat[:kv_local] = jnp.full((kv_local, rows), -jnp.inf, jnp.float32)
    stat[kv_local:] = jnp.zeros((kv_local, rows), jnp.float32)
    scale = head_dim ** -0.5 * math.log2(math.e)

    def receive_and_forward(dx, dy):
        slot = slot_of(dx, dy)
        for kind in range(2):
            ref = kv_buf.at[slot, pl.ds(kind * (kv_local // 2), kv_local // 2)]
            pltpu.make_async_remote_copy(
                src_ref=ref, dst_ref=ref, send_sem=kv_send, recv_sem=kv_recv.at[slot, kind],
                device_id={"core": other}, device_id_type=MESH).wait_recv()
            along, across = (dx, dy) if kind == 0 else (dy, dx)

            def step(sign, first_axis):
                on_x = (kind == 0) == first_axis
                return chip(sign % nx, 0) if on_x else chip(0, sign % ny)

            if across == 0:
                send(slot, kind, None, step(1, False))
                send(slot, kind, None, step(-1, False))
                if along == 3:
                    send(slot, kind, 0, step(1, True))
                if along == 1:
                    send(slot, kind, 1, step(-1, True))
            if across == 3:
                send(slot, kind, 0, step(1, False))
            if across == 1:
                send(slot, kind, 1, step(-1, False))

    def block_step(n, carry):
        slot = mine
        for k, (dx, dy) in enumerate(ORDER):
            if k == 0:
                continue
            slot = jnp.where(n == k, slot_of(dx, dy), slot)

            @pl.when(n + 1 == k)
            def _():
                receive_and_forward(dx, dy)

        for h in range(kv_local):
            kv = kv_buf[slot, h]
            v_t = jnp.transpose(kv.astype(jnp.float32), (1, 0))[head_dim:].astype(jnp.bfloat16)
            for t in range(rows // TILE):
                cols = slice(t * TILE, (t + 1) * TILE)
                scores = jnp.dot(kv, q_t[h, :, cols], preferred_element_type=jnp.float32)
                old_max = stat[h:h + 1, cols]
                new_max = jnp.maximum(old_max, jnp.max(scores, axis=0, keepdims=True))
                rescale = jnp.exp2((old_max - new_max) * scale)
                weights = jnp.exp2((scores - new_max) * scale)
                stat[h:h + 1, cols] = new_max
                stat[kv_local + h:kv_local + h + 1, cols] = (
                    stat[kv_local + h:kv_local + h + 1, cols] * rescale + jnp.sum(weights, axis=0, keepdims=True))
                acc[h, :, cols] = acc[h, :, cols] * rescale + jnp.dot(
                    v_t, weights.astype(jnp.bfloat16), preferred_element_type=jnp.float32)
        return carry

    lax.fori_loop(0, len(ORDER), block_step, 0)

    for h in range(kv_local):
        out = acc[h] / stat[kv_local + h:kv_local + h + 1, :]
        for pair in range(group // 2):
            cols = slice(h * q_rows + pair * LANES, h * q_rows + (pair + 1) * LANES)
            first = 2 * pair * LANES
            both = jnp.concatenate([out[:, first:first + LANES], out[:, first + LANES:first + 2 * LANES]], axis=0)
            o_buf[:main, cols] = jnp.transpose(both, (1, 0)).astype(jnp.bfloat16)
            ends = out[:, (group + pair) * LANES:(group + pair + 1) * LANES]
            both = jnp.concatenate([ends, pltpu.roll(ends, tail, 1)], axis=0)
            o_buf[main:, cols] = jnp.transpose(both, (1, 0))[:tail].astype(jnp.bfloat16)

    o_copy = pltpu.make_async_remote_copy(
        src_ref=o_buf.at[other_rows], dst_ref=o_recv, send_sem=o_sem.at[0], recv_sem=o_sem.at[1],
        device_id={"core": other}, device_id_type=MESH)
    o_copy.start()
    o_load.wait()
    y = jnp.dot(o_buf[own_rows], w_o[pl.ds(pl.multiple_of(core * feat, feat), feat)],
                preferred_element_type=jnp.float32)
    o_copy.wait()
    y = y + jnp.dot(o_recv[...], w_o[pl.ds(pl.multiple_of(other * feat, feat), feat)],
                    preferred_element_type=jnp.float32)
    y_ref[...] = y.astype(jnp.bfloat16)

    sent = kv_buf.at[pl.ds(0, nx * ny - 1)]
    pltpu.make_async_remote_copy(
        src_ref=sent, dst_ref=sent, send_sem=kv_send, recv_sem=o_sem.at[1],
        device_id={"core": other}, device_id_type=MESH).wait_send()


def solution(mesh):
    nx, ny = mesh.shape["cx"], mesh.shape["cy"]
    seq_spec = P("dp", ("cy", "cx", "core"))

    def local_layer(x_loc, w_qkv, w_out):
        heads, head_dim, width = w_out.shape
        kv_heads = (w_qkv.shape[1] - heads) // 2
        tokens = x_loc.shape[1]
        kv_local = kv_heads // 2
        group = heads // kv_heads
        feat = kv_local * group * head_dim
        rows = group * 2 * tokens
        dims = (nx, ny, heads, kv_heads, head_dim)
        w_rows = jnp.transpose(w_qkv, (1, 2, 0)).reshape(-1, width)
        hbm = pl.BlockSpec(memory_space=pl.ANY)
        y = pl.pallas_call(
            functools.partial(kernel, dims),
            out_shape=jax.ShapeDtypeStruct((tokens, width), jnp.bfloat16),
            in_specs=[hbm] * 3,
            out_specs=pl.BlockSpec(memory_space=pltpu.VMEM),
            scratch_shapes=[
                pltpu.VMEM((TILE, width), jnp.bfloat16),
                pltpu.VMEM((2 * kv_local * head_dim, width), jnp.bfloat16),
                pltpu.VMEM((feat, width), jnp.bfloat16),
                pltpu.VMEM((heads * head_dim, width), jnp.bfloat16),
                pltpu.VMEM((nx * ny, kv_local, 2 * tokens, LANES), jnp.bfloat16),
                pltpu.VMEM((kv_local, LANES, rows), jnp.bfloat16),
                pltpu.VMEM((kv_local, head_dim, rows), jnp.float32),
                pltpu.VMEM((2 * kv_local, rows), jnp.float32),
                pltpu.VMEM((2 * tokens, feat), jnp.bfloat16),
                pltpu.VMEM((tokens, feat), jnp.bfloat16),
                pltpu.SemaphoreType.DMA((3 + 2 * kv_local,)),
                pltpu.SemaphoreType.DMA((2,)),
                pltpu.SemaphoreType.DMA,
                pltpu.SemaphoreType.DMA((nx * ny, 2)),
                pltpu.SemaphoreType.DMA((2,)),
            ],
            compiler_params=pltpu.CompilerParams(collective_id=0, has_side_effects=True),
        )(x_loc[0], w_rows, w_out.reshape(heads * head_dim, width))
        return y[None]

    return jax.shard_map(local_layer, mesh=mesh, in_specs=(seq_spec, P(), P()), out_specs=seq_spec, check_vma=False)
```

time: 93.4 us -> 73.3 us (0.78)
  Pallas kernels: 0 us -> 71.4 us
  blocking collectives: 52.1 us -> 0 us
  matrix products: 24.8 us -> 0 us
  local copies, waits for them, and re-layouts: 8.99 us -> 1.77 us
  other arithmetic: 6.83 us -> 0 us
    pallas_call x0 -> x1, Pallas kernels: none -> 71.4 us  [local_layer(): pl.pallas_call(functools.partial(kernel, dims), out_shape=jax.ShapeDtypeS...]
    all_to_all x4 -> x0, blocking collectives: 38.1 us -> none  [the longest x1 16.3 us: local_layer(): packed = lax.all_to_all(packed, 'cx', 1, 0, tiled=True)]
    dot_general x9 -> x0, matrix products: 18.4 us -> none  [the longest x4 7.02 us: local_layer(): jnp.einsum('kgqs,skd->kgqd', weights.astype(jnp.bfloat16), v_block, prefe...]
    all_gather x1 -> x0, blocking collectives: 14 us -> none  [local_layer(): kv_all = lax.all_gather(packed[:, 0, q_local:], 'cy')]
    reduce_sum x2 -> x0, other arithmetic: 6.48 us -> none  [local_layer(): run_sum = run_sum * rescale + weights.sum(axis=-1)]
    unnamed x1 -> x0, matrix products: 6.46 us -> none
    all_to_all x8 -> x0, local copies, waits for them, and re-layouts: 3.28 us -> none  [the longest x3 1.33 us: local_layer(): attn_out = lax.all_to_all(attn_out, 'core', 0, 1, tiled=True)]
    unnamed x8 -> x1, local copies, waits for them, and re-layouts: 3.34 us -> 1.77 us
where the time goes in v1:
time: 73.3 us; the launch traced here: 73.2 us
  Pallas kernels  71.4 us (97%)
  local copies, waits for them, and re-layouts  1.77 us (2%)
    pallas_call x1, Pallas kernels, local_layer(): pl.pallas_call(functools.partial(kernel, dims), out_shape=jax.ShapeDtypeS...  71.4 us
    unnamed x1, local copies, waits for them, and re-layouts  1.77 us

profile of v1, /device:TPU:97, one launch (start us, length us, event | category | flops | bytes accessed | tf_op | source)
XLA Modules:
  0.0 73.2 jit_solution(12890829936643541130)
XLA Ops:
  0.0 71.4 %shard_map.37 = bf16[96,2048]{1,0:T(8,128)(2,1)} custom-call(bf16[96,2048]{1,0:T(8,128)(2,1)} %bitcast.9, bf16[3072,2048]{1,0:T(8,128)(2,1)} %bitcast.6, bf16[2048,2048]{1,0:T(8,128)(2,1)} %bitcast.7), custom_call_target="tpu_custom_call" | custom-call | tf_op jit(solution)/shard_map/pallas_call | solution.py:223
  71.4 1.8 %copy.5 = bf16[1,96,2048]{2,1,0:T(8,128)(2,1)} copy(bf16[1,96,2048]{2,1,0:T(8,128)(2,1)} %bitcast.8) | data formatting | bytes 786432

commit v2 on v1

--- a/solution.py
+++ b/solution.py
@@ -23,7 +23,7 @@
 
 
 def kernel(dims, x_hbm, wqkv_hbm, wout_hbm, y_ref,
-           x_ext, w_kv, w_q, w_o, kv_buf, q_t, acc, stat, o_buf, o_recv,
+           x_ext, w_kv, w_q, w_o, kv_buf, q_t, v_t, s_buf, acc, stat, o_buf, o_recv,
            load_sem, x_sem, kv_send, kv_recv, o_sem):
     nx, ny, heads, kv_heads, head_dim = dims
     chip_tokens = o_buf.shape[0]
@@ -118,7 +118,7 @@
 
     acc[...] = jnp.zeros_like(acc)
     stat[:kv_local] = jnp.full((kv_local, rows), -jnp.inf, jnp.float32)
-    stat[kv_local:] = jnp.zeros((kv_local, rows), jnp.float32)
+    stat[kv_local:2 * kv_local] = jnp.zeros((kv_local, rows), jnp.float32)
     scale = head_dim ** -0.5 * math.log2(math.e)
 
     def receive_and_forward(dx, dy):
@@ -146,6 +146,36 @@
             if across == 1:
                 send(slot, kind, 1, step(-1, False))
 
+    tiles = rows // TILE
+
+    def score(slot):
+        def head_tile(h, t):
+            cols = slice(t * TILE, (t + 1) * TILE)
+            if t == 0:
+                v_t[h] = jnp.transpose(kv_buf[slot, h].astype(jnp.float32), (1, 0))[head_dim:].astype(jnp.bfloat16)
+            scores = jnp.dot(kv_buf[slot, h], q_t[h, :, cols], preferred_element_type=jnp.float32)
+            old_max = stat[h:h + 1, cols]
+            new_max = jnp.maximum(old_max, jnp.max(scores, axis=0, keepdims=True))
+            stat[h:h + 1, cols] = new_max
+            stat[2 * kv_local + h:2 * kv_local + h + 1, cols] = jnp.exp2((old_max - new_max) * scale)
+            s_buf[h * tiles + t] = scores
+        return head_tile
+
+    def absorb(h, t):
+        cols = slice(t * TILE, (t + 1) * TILE)
+        rescale = stat[2 * kv_local + h:2 * kv_local + h + 1, cols]
+        weights = jnp.exp2((s_buf[h * tiles + t] - stat[h:h + 1, cols]) * scale)
+        stat[kv_local + h:kv_local + h + 1, cols] = (
+            stat[kv_local + h:kv_local + h + 1, cols] * rescale + jnp.sum(weights, axis=0, keepdims=True))
+        acc[h, :, cols] = acc[h, :, cols] * rescale + jnp.dot(
+            v_t[h], weights.astype(jnp.bfloat16), preferred_element_type=jnp.float32)
+
+    pieces = [(h, t) for h in range(kv_local) for t in range(tiles)]
+
+    first_score = score(mine)
+    for h, t in pieces:
+        first_score(h, t)
+
     def block_step(n, carry):
         slot = mine
         for k, (dx, dy) in enumerate(ORDER):
@@ -153,28 +183,21 @@
                 continue
             slot = jnp.where(n == k, slot_of(dx, dy), slot)
 
-            @pl.when(n + 1 == k)
+            @pl.when(n == k)
             def _():
                 receive_and_forward(dx, dy)
 
-        for h in range(kv_local):
-            kv = kv_buf[slot, h]
-            v_t = jnp.transpose(kv.astype(jnp.float32), (1, 0))[head_dim:].astype(jnp.bfloat16)
-            for t in range(rows // TILE):
-                cols = slice(t * TILE, (t + 1) * TILE)
-                scores = jnp.dot(kv, q_t[h, :, cols], preferred_element_type=jnp.float32)
-                old_max = stat[h:h + 1, cols]
-                new_max = jnp.maximum(old_max, jnp.max(scores, axis=0, keepdims=True))
-                rescale = jnp.exp2((old_max - new_max) * scale)
-                weights = jnp.exp2((scores - new_max) * scale)
-                stat[h:h + 1, cols] = new_max
-                stat[kv_local + h:kv_local + h + 1, cols] = (
-                    stat[kv_local + h:kv_local + h + 1, cols] * rescale + jnp.sum(weights, axis=0, keepdims=True))
-                acc[h, :, cols] = acc[h, :, cols] * rescale + jnp.dot(
-                    v_t, weights.astype(jnp.bfloat16), preferred_element_type=jnp.float32)
+        next_score = score(slot)
+        for i, (h, t) in enumerate(pieces):
+            absorb(h, t)
+            if t == tiles - 1:
+                for u in range(tiles):
+                    next_score(h, u)
         return carry
 
-    lax.fori_loop(0, len(ORDER), block_step, 0)
+    lax.fori_loop(1, len(ORDER), block_step, 0)
+    for h, t in pieces:
+        absorb(h, t)
 
     for h in range(kv_local):
         out = acc[h] / stat[kv_local + h:kv_local + h + 1, :]
@@ -232,8 +255,10 @@
                 pltpu.VMEM((heads * head_dim, width), jnp.bfloat16),
                 pltpu.VMEM((nx * ny, kv_local, 2 * tokens, LANES), jnp.bfloat16),
                 pltpu.VMEM((kv_local, LANES, rows), jnp.bfloat16),
+                pltpu.VMEM((kv_local, head_dim, 2 * tokens), jnp.bfloat16),
+                pltpu.VMEM((kv_local * (rows // TILE), 2 * tokens, TILE), jnp.float32),
                 pltpu.VMEM((kv_local, head_dim, rows), jnp.float32),
-                pltpu.VMEM((2 * kv_local, rows), jnp.float32),
+                pltpu.VMEM((3 * kv_local, rows), jnp.float32),
                 pltpu.VMEM((2 * tokens, feat), jnp.bfloat16),
                 pltpu.VMEM((tokens, feat), jnp.bfloat16),
                 pltpu.SemaphoreType.DMA((3 + 2 * kv_local,)),

time: 73.3 us -> 43.1 us (0.59)
  Pallas kernels: 71.4 us -> 41.2 us
    pallas_call x1, Pallas kernels: 71.4 us -> 41.2 us  [local_layer(): pl.pallas_call(functools.partial(kernel, dims), out_shape=jax.ShapeDtypeS...]
where the time goes in v2:
time: 43.1 us; the launch traced here: 42.9 us
  Pallas kernels  41.2 us (96%)
  local copies, waits for them, and re-layouts  1.77 us (4%)
    pallas_call x1, Pallas kernels, local_layer(): pl.pallas_call(functools.partial(kernel, dims), out_shape=jax.ShapeDtypeS...  41.2 us
    unnamed x1, local copies, waits for them, and re-layouts  1.77 us

profile of v2, /device:TPU:97, one launch (start us, length us, event | category | flops | bytes accessed | tf_op | source)
XLA Modules:
  0.0 42.9 jit_solution(16381560369496498528)
XLA Ops:
  0.0 41.2 %shard_map.37 = bf16[96,2048]{1,0:T(8,128)(2,1)} custom-call(bf16[96,2048]{1,0:T(8,128)(2,1)} %bitcast.9, bf16[3072,2048]{1,0:T(8,128)(2,1)} %bitcast.6, bf16[2048,2048]{1,0:T(8,128)(2,1)} %bitcast.7), custom_call_target="tpu_custom_call" | custom-call | tf_op jit(solution)/shard_map/pallas_call | solution.py:246
  41.2 1.8 %copy.5 = bf16[1,96,2048]{2,1,0:T(8,128)(2,1)} copy(bf16[1,96,2048]{2,1,0:T(8,128)(2,1)} %bitcast.8) | data formatting | bytes 786432

commit v3 on v2

--- a/solution.py
+++ b/solution.py
@@ -16,8 +16,8 @@
 ORDER = (
     (0, 0),
     (1, 0), (3, 0), (0, 1), (0, 3),
-    (2, 0), (0, 2), (1, 1), (3, 3), (1, 3), (3, 1),
-    (2, 1), (1, 2), (2, 3), (3, 2),
+    (2, 0), (1, 1), (3, 1), (1, 3), (0, 2), (3, 3),
+    (2, 1), (2, 3), (1, 2), (3, 2),
     (2, 2),
 )
 
@@ -89,13 +89,12 @@
         return lax.rem(cy + dy, ny) * nx + lax.rem(cx + dx, nx)
 
     mine = slot_of(0, 0)
+    for copy in kv_loads:
+        copy.wait()
+    part = lax.dot_general(x_ext[:chip_tokens], w_kv[...], NT, preferred_element_type=jnp.float32)
+    for h in range(kv_local):
+        kv_buf[mine, h] = part[:, h * LANES:(h + 1) * LANES].astype(jnp.bfloat16)
     for kind in range(2):
-        for copy in kv_loads[kind * kv_local:(kind + 1) * kv_local]:
-            copy.wait()
-        part = lax.dot_general(
-            x_ext[:chip_tokens], w_kv[kind * TILE:(kind + 1) * TILE], NT, preferred_element_type=jnp.float32)
-        for h in range(2):
-            kv_buf[mine, kind * 2 + h] = part[:, h * LANES:(h + 1) * LANES].astype(jnp.bfloat16)
         for target in (chip(1, 0), chip(nx - 1, 0), chip(0, 1), chip(0, ny - 1)):
             send(mine, kind, None, target)
 
@@ -121,35 +120,35 @@
     stat[kv_local:2 * kv_local] = jnp.zeros((kv_local, rows), jnp.float32)
     scale = head_dim ** -0.5 * math.log2(math.e)
 
-    def receive_and_forward(dx, dy):
+    def receive_and_forward(kind, along, across):
+        dx, dy = (along, across) if kind == 0 else (across, along)
         slot = slot_of(dx, dy)
-        for kind in range(2):
-            ref = kv_buf.at[slot, pl.ds(kind * (kv_local // 2), kv_local // 2)]
-            pltpu.make_async_remote_copy(
-                src_ref=ref, dst_ref=ref, send_sem=kv_send, recv_sem=kv_recv.at[slot, kind],
-                device_id={"core": other}, device_id_type=MESH).wait_recv()
-            along, across = (dx, dy) if kind == 0 else (dy, dx)
-
-            def step(sign, first_axis):
-                on_x = (kind == 0) == first_axis
-                return chip(sign % nx, 0) if on_x else chip(0, sign % ny)
-
-            if across == 0:
-                send(slot, kind, None, step(1, False))
-                send(slot, kind, None, step(-1, False))
-                if along == 3:
-                    send(slot, kind, 0, step(1, True))
-                if along == 1:
-                    send(slot, kind, 1, step(-1, True))
-            if across == 3:
-                send(slot, kind, 0, step(1, False))
-            if across == 1:
-                send(slot, kind, 1, step(-1, False))
+        ref = kv_buf.at[slot, pl.ds(kind * (kv_local // 2), kv_local // 2)]
+        pltpu.make_async_remote_copy(
+            src_ref=ref, dst_ref=ref, send_sem=kv_send, recv_sem=kv_recv.at[slot, kind],
+            device_id={"core": other}, device_id_type=MESH).wait_recv()
+
+        def step(sign, first_axis):
+            on_x = (kind == 0) == first_axis
+            return chip(sign % nx, 0) if on_x else chip(0, sign % ny)
+
+        if across == 0:
+            if along == 3:
+                send(slot, kind, 0, step(1, True))
+            if along == 1:
+                send(slot, kind, 1, step(-1, True))
+            send(slot, kind, None, step(1, False))
+            send(slot, kind, None, step(-1, False))
+        if across == 3:
+            send(slot, kind, 0, step(1, False))
+        if across == 1:
+            send(slot, kind, 1, step(-1, False))
 
     tiles = rows // TILE
 
-    def score(slot):
+    def score(slots):
         def head_tile(h, t):
+            slot = slots[h * 2 // kv_local]
             cols = slice(t * TILE, (t + 1) * TILE)
             if t == 0:
                 v_t[h] = jnp.transpose(kv_buf[slot, h].astype(jnp.float32), (1, 0))[head_dim:].astype(jnp.bfloat16)
@@ -172,22 +171,24 @@
 
     pieces = [(h, t) for h in range(kv_local) for t in range(tiles)]
 
-    first_score = score(mine)
+    first_score = score((mine, mine))
     for h, t in pieces:
         first_score(h, t)
 
     def block_step(n, carry):
-        slot = mine
-        for k, (dx, dy) in enumerate(ORDER):
+        slots = [mine, mine]
+        for k, (along, across) in enumerate(ORDER):
             if k == 0:
                 continue
-            slot = jnp.where(n == k, slot_of(dx, dy), slot)
+            slots[0] = jnp.where(n == k, slot_of(along, across), slots[0])
+            slots[1] = jnp.where(n == k, slot_of(across, along), slots[1])
 
             @pl.when(n == k)
             def _():
-                receive_and_forward(dx, dy)
-
-        next_score = score(slot)
+                receive_and_forward(0, along, across)
+                receive_and_forward(1, along, across)
+
+        next_score = score(slots)
         for i, (h, t) in enumerate(pieces):
             absorb(h, t)
             if t == tiles - 1:
@@ -267,7 +268,8 @@
                 pltpu.SemaphoreType.DMA((nx * ny, 2)),
                 pltpu.SemaphoreType.DMA((2,)),
             ],
-            compiler_params=pltpu.CompilerParams(collective_id=0, has_side_effects=True),
+            compiler_params=pltpu.CompilerParams(
+                collective_id=0, has_side_effects=True, vmem_limit_bytes=54000 * 1024),
         )(x_loc[0], w_rows, w_out.reshape(heads * head_dim, width))
         return y[None]
 

time: 43.1 us -> 40.5 us (0.940)
  Pallas kernels: 41.2 us -> 38.6 us
    pallas_call x1, Pallas kernels: 41.2 us -> 38.6 us  [local_layer(): pl.pallas_call(functools.partial(kernel, dims), out_shape=jax.ShapeDtypeS...]
    unnamed x1 -> x3, local copies, waits for them, and re-layouts: 1.77 us -> 1.74 us
where the time goes in v3:
time: 40.5 us; the launch traced here: 40.4 us
  Pallas kernels  38.6 us (95%)
  local copies, waits for them, and re-layouts  1.74 us (4%)
    pallas_call x1, Pallas kernels, local_layer(): pl.pallas_call(functools.partial(kernel, dims), out_shape=jax.ShapeDtypeS...  38.6 us
    unnamed x3, local copies, waits for them, and re-layouts  1.74 us

profile of v3, /device:TPU:97, one launch (start us, length us, event | category | flops | bytes accessed | tf_op | source)
XLA Modules:
  0.0 40.4 jit_solution(9589765253328272298)
XLA Ops:
  0.0 0.0 copy-start
  0.0 1.0 %copy-done = bf16[1,96,2048]{2,1,0:T(8,128)(2,1)S(1)} copy-done((bf16[1,96,2048]{2,1,0:T(8,128)(2,1)S(1)}, bf16[1,96,2048]{2,1,0:T(8,128)(2,1)}, u32[]{:S(2)}) %copy-start) | copy-done | bytes 393240
  1.0 38.6 %shard_map.37 = bf16[96,2048]{1,0:T(8,128)(2,1)S(1)} custom-call(bf16[96,2048]{1,0:T(8,128)(2,1)S(1)} %bitcast.7, bf16[3072,2048]{1,0:T(8,128)(2,1)} %bitcast.8, bf16[2048,2048]{1,0:T(8,128)(2,1)} %bitcast.9), custom_call_target="tpu_custom_call" | custom-call | tf_op jit(solution)/shard_map/pallas_call | solution.py:247
  39.6 0.7 %copy.5 = bf16[1,96,2048]{2,1,0:T(8,128)(2,1)} copy(bf16[1,96,2048]{2,1,0:T(8,128)(2,1)S(1)} %bitcast.6) | data formatting | bytes 786432
Async XLA Ops:
  0.0 1.0 %copy-start = (bf16[1,96,2048]{2,1,0:T(8,128)(2,1)S(1)}, bf16[1,96,2048]{2,1,0:T(8,128)(2,1)}, u32[]{:S(2)}) copy-start(bf16[1,96,2048]{2,1,0:T(8,128)(2,1)} %param.3) | copy-start | bytes 1179652

commit v4 on v0

v4 whole, which is shorter than its diff:
```python
import functools
import math

import jax
import jax.numpy as jnp
from jax import lax
from jax.experimental import pallas as pl
from jax.experimental.pallas import tpu as pltpu
from jax.sharding import PartitionSpec as P

MESH = pl.DeviceIdType.MESH
LANES = 128
TILE = 256
NT = (((1,), (1,)), ((), ()))

STEPS = (
    (0, 0), (1, 0), (3, 0), (2, 0), (2, 1), (2, 3), (1, 1), (2, 2),
    (1, 3), (1, 2), (3, 1), (3, 3), (3, 2), (0, 1), (0, 3), (0, 2),
)


def kernel(dims, x_hbm, wqkv_hbm, wout_hbm, y_ref,
           x_ext, w_kv, w_q, w_o, kv_all, kv_buf, kv_relay, q_all, q_t, q_relay,
           v_t, s_buf, m_cur, r_cur, m_run, l_run, acc, o_send, o_relay, o_all, y_acc,
           load_sem, x_sem, kv_send, kv_recv, kv_relay_sem, q_send, q_recv, q_relay_sem,
           o_send_sem, o_recv, o_relay_sem):
    nx, ny, heads, kv_heads, head_dim = dims
    chip_tokens = kv_all.shape[1]
    dev_tokens = chip_tokens // 2
    kv_local = kv_heads // 2
    group = heads // kv_heads
    q_rows = group * head_dim
    feat = kv_local * q_rows
    rows = q_t.shape[2]
    tiles = rows // TILE
    main = LANES
    tail = chip_tokens - main
    cx, cy, core = lax.axis_index("cx"), lax.axis_index("cy"), lax.axis_index("core")
    other = 1 - core
    own_rows = pl.ds(pl.multiple_of(core * dev_tokens, 32), dev_tokens)
    other_rows = pl.ds(pl.multiple_of(other * dev_tokens, 32), dev_tokens)
    scale = head_dim ** -0.5 * math.log2(math.e)

    x_load = pltpu.make_async_copy(x_hbm, x_ext.at[own_rows], load_sem.at[0])
    x_load.start()
    kv_loads = []
    for h in range(kv_local):
        head = core * kv_local + h
        for part in range(2):
            src = pl.multiple_of((heads + part * kv_heads + head) * head_dim, head_dim)
            copy = pltpu.make_async_copy(
                wqkv_hbm.at[pl.ds(src, head_dim)],
                w_kv.at[pl.ds(h * 2 * head_dim + part * head_dim, head_dim)],
                load_sem.at[1 + 2 * h + part])
            copy.start()
            kv_loads.append(copy)
    q_load = pltpu.make_async_copy(
        wqkv_hbm.at[pl.ds(pl.multiple_of(core * feat, feat), feat)], w_q, load_sem.at[1 + 2 * kv_local])
    q_load.start()

    east = {"cx": lax.rem(cx + 1, nx)}
    west = {"cx": lax.rem(cx + nx - 1, nx)}
    north = {"cy": lax.rem(cy + 1, ny)}
    south = {"cy": lax.rem(cy + ny - 1, ny)}
    partner = {"core": other}
    targets = (partner, east, west, {**east, **partner}, {**west, **partner}, north, south)
    barrier = pltpu.get_barrier_semaphore()
    for target in targets:
        pl.semaphore_signal(barrier, inc=1, device_id=target, device_id_type=MESH)
    pl.semaphore_wait(barrier, len(targets))

    def remote(src, dst, send_sem, recv_sem, target):
        return pltpu.make_async_remote_copy(
            src_ref=src, dst_ref=dst, send_sem=send_sem, recv_sem=recv_sem, device_id=target, device_id_type=MESH)

    x_load.wait()
    x_copy = remote(x_ext.at[own_rows], x_ext.at[own_rows], x_sem.at[0], x_sem.at[1], partner)
    x_copy.start()
    q_t[:, head_dim:, :] = jnp.zeros((nx, LANES - head_dim, rows), jnp.bfloat16)
    acc[...] = jnp.zeros_like(acc)
    m_run[...] = jnp.full_like(m_run, -jnp.inf)
    l_run[...] = jnp.zeros_like(l_run)
    for copy in kv_loads:
        copy.wait()
    x_copy.wait()

    part = lax.dot_general(x_ext[:chip_tokens], w_kv[...], NT, preferred_element_type=jnp.float32)
    for h in range(kv_local):
        kv_all[h] = part[:, h * LANES:(h + 1) * LANES].astype(jnp.bfloat16)

    def head_at(dx):
        return lax.rem(cx + dx, nx)

    def kv_piece(dx, dy):
        return kv_buf.at[dy, pl.ds(dx * chip_tokens, chip_tokens)]

    def kv_half(dx, half):
        return kv_buf.at[0, pl.ds(dx * chip_tokens + half * dev_tokens, dev_tokens)]

    far = kv_all.at[head_at(2)]
    for half, target in ((0, east), (1, west)):
        remote(far.at[pl.ds(half * dev_tokens, dev_tokens)], kv_relay.at[half],
               kv_send, kv_relay_sem.at[half], target).start()
    remote(kv_all.at[head_at(1)], kv_piece(3, 0), kv_send, kv_recv.at[0, 3], east).start()
    remote(kv_all.at[head_at(3)], kv_piece(1, 0), kv_send, kv_recv.at[0, 1], west).start()

    def spread(src, dx):
        remote(src, kv_piece(dx, 3), kv_send, kv_recv.at[3, dx], north).start()
        remote(src, kv_piece(dx, 1), kv_send, kv_recv.at[1, dx], south).start()

    spread(kv_all.at[cx], 0)
    kv_buf[0, :chip_tokens] = kv_all[cx]
    o_load = pltpu.make_async_copy(wout_hbm, w_o, load_sem.at[2 + 2 * kv_local])
    o_load.start()

    q_load.wait()
    x_ext[chip_tokens:chip_tokens + tail] = x_ext[main:chip_tokens]
    lane = lax.broadcasted_iota(jnp.int32, (head_dim, LANES), 1)
    for dx in (2, 1, 3, 0):
        res = lax.dot_general(
            w_q[pl.ds(pl.multiple_of(head_at(dx) * q_rows, q_rows), q_rows)], x_ext[...], NT,
            preferred_element_type=jnp.float32)
        dst = q_t.at[0, pl.ds(0, head_dim)] if dx == 0 else q_all.at[dx]
        for g in range(group):
            dst[:, g * LANES:(g + 1) * LANES] = res[g * head_dim:(g + 1) * head_dim, :main].astype(jnp.bfloat16)
        for pair in range(group // 2):
            lo = res[2 * pair * head_dim:(2 * pair + 1) * head_dim, main:]
            hi = res[(2 * pair + 1) * head_dim:(2 * pair + 2) * head_dim, main:]
            dst[:, (group + pair) * LANES:(group + pair + 1) * LANES] = (
                jnp.where(lane < tail, lo, hi).astype(jnp.bfloat16))
        half_dim = head_dim // 2
        if dx == 2:
            for half, target in ((0, east), (1, west)):
                remote(q_all.at[2, pl.ds(half * half_dim, half_dim)], q_relay.at[half],
                       q_send, q_relay_sem.at[half], target).start()
        if dx == 1:
            remote(q_all.at[1], q_t.at[3, pl.ds(0, head_dim)], q_send, q_recv.at[3], east).start()
        if dx == 3:
            remote(q_all.at[3], q_t.at[1, pl.ds(0, head_dim)], q_send, q_recv.at[1], west).start()

    def arrive(ref, sem):
        remote(ref, ref, kv_send, sem, partner).wait_recv()

    def kv_relay_on():
        for half, target in ((0, east), (1, west)):
            arrive(kv_relay.at[half], kv_relay_sem.at[half])
            remote(kv_relay.at[half], kv_half(2, half), kv_send, kv_recv.at[0, 2], target).start()

    def kv_row(dx):
        arrive(kv_piece(dx, 0), kv_recv.at[0, dx])
        spread(kv_piece(dx, 0), dx)

    def kv_side(dx, dy):
        arrive(kv_piece(dx, dy), kv_recv.at[dy, dx])
        if dy == 3 and dx % 2 == 0:
            remote(kv_piece(dx, 3), kv_piece(dx, 2), kv_send, kv_recv.at[2, dx], north).start()
        if dy == 1 and dx % 2 == 1:
            remote(kv_piece(dx, 1), kv_piece(dx, 2), kv_send, kv_recv.at[2, dx], south).start()

    def q_relay_on():
        for half, target in ((0, east), (1, west)):
            arrive(q_relay.at[half], q_relay_sem.at[half])
            remote(q_relay.at[half], q_t.at[2, pl.ds(half * half_dim, half_dim)],
                   q_send, q_recv.at[2], target).start()

    def q_arrive(dx):
        arrive(q_t.at[dx, pl.ds(0, head_dim)], q_recv.at[dx])

    def o_relay_on():
        for half, target in ((0, east), (1, {**west, **partner})):
            arrive(o_relay.at[half], o_relay_sem.at[half])
            remote(o_relay.at[half], o_all.at[half, 2], o_send_sem.at[0], o_recv.at[half, 2], target).start()

    def score(q, dy, t):
        cols = slice(t * TILE, (t + 1) * TILE)
        scores = jnp.dot(kv_buf[dy], q_t[q, :, cols], preferred_element_type=jnp.float32)
        old_max = m_run[q, :, cols]
        new_max = jnp.maximum(old_max, jnp.max(scores, axis=0, keepdims=True))
        m_run[q, :, cols] = new_max
        m_cur[:, cols] = new_max
        r_cur[:, cols] = jnp.exp2((old_max - new_max) * scale)
        s_buf[t] = scores

    def absorb(q, dy, t):
        cols = slice(t * TILE, (t + 1) * TILE)
        rescale = r_cur[:, cols]
        weights = jnp.exp2((s_buf[t] - m_cur[:, cols]) * scale)
        l_run[q, :, cols] = l_run[q, :, cols] * rescale + jnp.sum(weights, axis=0, keepdims=True)
        acc[q, :, cols] = acc[q, :, cols] * rescale + jnp.dot(
            v_t[dy], weights.astype(jnp.bfloat16), preferred_element_type=jnp.float32)

    def finish(q):
        out = acc[q] / l_run[q]
        dst = o_send.at[q]
        for pair in range(group // 2):
            cols = slice(pair * LANES, (pair + 1) * LANES)
            first = 2 * pair * LANES
            both = jnp.concatenate([out[:, first:first + LANES], out[:, first + LANES:first + 2 * LANES]], axis=0)
            dst[:main, cols] = jnp.transpose(both, (1, 0)).astype(jnp.bfloat16)
            ends = out[:, (group + pair) * LANES:(group + pair + 1) * LANES]
            both = jnp.concatenate([ends, pltpu.roll(ends, tail, 1)], axis=0)
            dst[main:, cols] = jnp.transpose(both, (1, 0))[:tail].astype(jnp.bfloat16)
        mine, theirs = o_send.at[q, own_rows], o_send.at[q, other_rows]
        if q == 2:
            remote(mine, o_relay.at[0], o_send_sem.at[0], o_relay_sem.at[0], east).start()
            remote(theirs, o_relay.at[1], o_send_sem.at[0], o_relay_sem.at[1], west).start()
        elif q:
            target = east if q == 1 else west
            remote(mine, o_all.at[0, nx - q], o_send_sem.at[0], o_recv.at[0, nx - q], target).start()
            remote(theirs, o_all.at[1, nx - q], o_send_sem.at[0], o_recv.at[1, nx - q], {**target, **partner}).start()
        else:
            remote(theirs, o_all.at[1, 0], o_send_sem.at[1], o_recv.at[1, 0], partner).start()
            o_all[0, 0] = o_send[0, own_rows]

    events = {n: [] for n in range(len(STEPS) + 1)}
    events[0] = [kv_relay_on, lambda: kv_row(1), lambda: kv_row(3), lambda: kv_side(0, 1), lambda: kv_side(0, 3),
                 lambda: kv_row(2), q_relay_on]
    events[1] = [lambda: kv_side(1, 1), lambda: kv_side(3, 1), lambda: kv_side(1, 3), lambda: kv_side(3, 3),
                 lambda: q_arrive(1)]
    events[2] = [lambda: q_arrive(3)]
    events[3] = [lambda: kv_side(2, 1), lambda: kv_side(2, 3), lambda: q_arrive(2)]
    events[7] = [lambda dx=dx: kv_side(dx, 2) for dx in range(nx)]
    events[12] = [o_relay_on]
    last_of = {q: max(n for n, s in enumerate(STEPS) if s[0] == q) for q in range(nx)}
    first_of = {dy: min(n for n, s in enumerate(STEPS) if s[1] == dy) for dy in range(ny)}

    for n in range(len(STEPS) + 1):
        for event in events[n]:
            event()
        if n < len(STEPS) and first_of[STEPS[n][1]] == n:
            dy = STEPS[n][1]
            v_t[dy] = jnp.transpose(kv_buf[dy].astype(jnp.float32), (1, 0))[head_dim:].astype(jnp.bfloat16)
        for t in range(tiles):
            if n:
                absorb(*STEPS[n - 1], t)
            if n < len(STEPS):
                score(*STEPS[n], t)
        if n and last_of[STEPS[n - 1][0]] == n - 1:
            finish(STEPS[n - 1][0])

    o_load.wait()
    for i, dx in enumerate((2, 1, 3, 0)):
        total = None
        for r in range(2):
            if dx or r:
                arrive(o_all.at[r, dx], o_recv.at[r, dx])
            first = ((core if r == 0 else other) * kv_local + head_at(dx)) * q_rows
            term = jnp.dot(o_all[r, dx], w_o[pl.ds(pl.multiple_of(first, q_rows), q_rows)],
                           preferred_element_type=jnp.float32)
            total = term if total is None else total + term
        if i == 0:
            y_acc[...] = total
        elif i < nx - 1:
            y_acc[...] += total
        else:
            y_ref[...] = (y_acc[...] + total).astype(jnp.bfloat16)

    for ref, sem in ((kv_buf, kv_send), (q_all, q_send), (o_all, o_send_sem.at[0]), (o_all.at[1, 0], o_send_sem.at[1])):
        remote(ref, ref, sem, x_sem.at[1], partner).wait_send()


def solution(mesh):
    nx, ny = mesh.shape["cx"], mesh.shape["cy"]
    seq_spec = P("dp", ("cy", "cx", "core"))

    def local_layer(x_loc, w_qkv, w_out):
        heads, head_dim, width = w_out.shape
        kv_heads = (w_qkv.shape[1] - heads) // 2
        tokens = x_loc.shape[1]
        kv_local = kv_heads // 2
        group = heads // kv_heads
        q_rows = group * head_dim
        feat = kv_local * q_rows
        rows = group * 2 * tokens
        dims = (nx, ny, heads, kv_heads, head_dim)
        w_rows = jnp.transpose(w_qkv, (1, 2, 0)).reshape(-1, width)
        hbm = pl.BlockSpec(memory_space=pl.ANY)
        half = jnp.bfloat16
        y = pl.pallas_call(
            functools.partial(kernel, dims),
            out_shape=jax.ShapeDtypeStruct((tokens, width), half),
            in_specs=[hbm] * 3,
            out_specs=pl.BlockSpec(memory_space=pltpu.VMEM),
            scratch_shapes=[
                pltpu.VMEM((TILE, width), half),
                pltpu.VMEM((2 * kv_local * head_dim, width), half),
                pltpu.VMEM((feat, width), half),
                pltpu.VMEM((heads * head_dim, width), half),
                pltpu.VMEM((kv_local, 2 * tokens, LANES), half),
                pltpu.VMEM((ny, nx * 2 * tokens, LANES), half),
                pltpu.VMEM((2, tokens, LANES), half),
                pltpu.VMEM((nx, head_dim, rows), half),
                pltpu.VMEM((nx, LANES, rows), half),
                pltpu.VMEM((2, head_dim // 2, rows), half),
                pltpu.VMEM((ny, head_dim, nx * 2 * tokens), half),
                pltpu.VMEM((rows // TILE, nx * 2 * tokens, TILE), jnp.float32),
                pltpu.VMEM((1, rows), jnp.float32),
                pltpu.VMEM((1, rows), jnp.float32),
                pltpu.VMEM((nx, 1, rows), jnp.float32),
                pltpu.VMEM((nx, 1, rows), jnp.float32),
                pltpu.VMEM((nx, head_dim, rows), jnp.float32),
                pltpu.VMEM((nx, 2 * tokens, q_rows), half),
                pltpu.VMEM((2, tokens, q_rows), half),
                pltpu.VMEM((2, nx, tokens, q_rows), half),
                pltpu.VMEM((tokens, width), jnp.float32),
                pltpu.SemaphoreType.DMA((3 + 2 * kv_local,)),
                pltpu.SemaphoreType.DMA((2,)),
                pltpu.SemaphoreType.DMA,
                pltpu.SemaphoreType.DMA((ny, nx)),
                pltpu.SemaphoreType.DMA((2,)),
                pltpu.SemaphoreType.DMA,
                pltpu.SemaphoreType.DMA((nx,)),
                pltpu.SemaphoreType.DMA((2,)),
                pltpu.SemaphoreType.DMA((2,)),
                pltpu.SemaphoreType.DMA((2, nx)),
                pltpu.SemaphoreType.DMA((2,)),
            ],
            compiler_params=pltpu.CompilerParams(
                collective_id=0, has_side_effects=True, vmem_limit_bytes=54000 * 1024),
        )(x_loc[0], w_rows, w_out.reshape(heads * head_dim, width))
        return y[None]

    return jax.shard_map(local_layer, mesh=mesh, in_specs=(seq_spec, P(), P()), out_specs=seq_spec, check_vma=False)
```

time: 93.4 us -> 38.8 us (0.42)
  blocking collectives: 52.1 us -> 0 us
  Pallas kernels: 0 us -> 36.9 us
  matrix products: 24.8 us -> 0 us
  local copies, waits for them, and re-layouts: 8.99 us -> 1.74 us
  other arithmetic: 6.83 us -> 0 us
    all_to_all x4 -> x0, blocking collectives: 38.1 us -> none  [the longest x1 16.3 us: local_layer(): packed = lax.all_to_all(packed, 'cx', 1, 0, tiled=True)]
    pallas_call x0 -> x1, Pallas kernels: none -> 36.9 us  [local_layer(): pl.pallas_call(functools.partial(kernel, dims), out_shape=jax.ShapeDtypeS...]
    dot_general x9 -> x0, matrix products: 18.4 us -> none  [the longest x4 7.02 us: local_layer(): jnp.einsum('kgqs,skd->kgqd', weights.astype(jnp.bfloat16), v_block, prefe...]
    all_gather x1 -> x0, blocking collectives: 14 us -> none  [local_layer(): kv_all = lax.all_gather(packed[:, 0, q_local:], 'cy')]
    reduce_sum x2 -> x0, other arithmetic: 6.48 us -> none  [local_layer(): run_sum = run_sum * rescale + weights.sum(axis=-1)]
    unnamed x1 -> x0, matrix products: 6.46 us -> none
    all_to_all x8 -> x0, local copies, waits for them, and re-layouts: 3.28 us -> none  [the longest x3 1.33 us: local_layer(): attn_out = lax.all_to_all(attn_out, 'core', 0, 1, tiled=True)]
    unnamed x8 -> x3, local copies, waits for them, and re-layouts: 3.34 us -> 1.74 us
where the time goes in v4:
time: 38.8 us; the launch traced here: 38.7 us
  Pallas kernels  36.9 us (95%)
  local copies, waits for them, and re-layouts  1.74 us (4%)
    pallas_call x1, Pallas kernels, local_layer(): pl.pallas_call(functools.partial(kernel, dims), out_shape=jax.ShapeDtypeS...  36.9 us
    unnamed x3, local copies, waits for them, and re-layouts  1.74 us

profile of v4, /device:TPU:97, one launch (start us, length us, event | category | flops | bytes accessed | tf_op | source)
XLA Modules:
  0.0 38.7 jit_solution(16184710251258255416)
XLA Ops:
  0.0 0.0 copy-start
  0.0 1.0 %copy-done = bf16[1,96,2048]{2,1,0:T(8,128)(2,1)S(1)} copy-done((bf16[1,96,2048]{2,1,0:T(8,128)(2,1)S(1)}, bf16[1,96,2048]{2,1,0:T(8,128)(2,1)}, u32[]{:S(2)}) %copy-start) | copy-done | bytes 393240
  1.0 36.9 %shard_map.37 = bf16[96,2048]{1,0:T(8,128)(2,1)S(1)} custom-call(bf16[96,2048]{1,0:T(8,128)(2,1)S(1)} %bitcast.7, bf16[3072,2048]{1,0:T(8,128)(2,1)} %bitcast.8, bf16[2048,2048]{1,0:T(8,128)(2,1)} %bitcast.9), custom_call_target="tpu_custom_call" | custom-call | tf_op jit(solution)/shard_map/pallas_call | solution.py:279
  38.0 0.7 %copy.5 = bf16[1,96,2048]{2,1,0:T(8,128)(2,1)} copy(bf16[1,96,2048]{2,1,0:T(8,128)(2,1)S(1)} %bitcast.6) | data formatting | bytes 786432
Async XLA Ops:
  0.0 1.0 %copy-start = (bf16[1,96,2048]{2,1,0:T(8,128)(2,1)S(1)}, bf16[1,96,2048]{2,1,0:T(8,128)(2,1)}, u32[]{:S(2)}) copy-start(bf16[1,96,2048]{2,1,0:T(8,128)(2,1)} %param.3) | copy-start | bytes 1179652

commit v5 on v4

v5 whole, which is shorter than its diff:
```python
import functools
import math

import jax
import jax.numpy as jnp
from jax import lax
from jax.experimental import pallas as pl
from jax.experimental.pallas import tpu as pltpu
from jax.sharding import PartitionSpec as P

MESH = pl.DeviceIdType.MESH
LANES = 128
TILE = 256
NT = (((1,), (1,)), ((), ()))

STEPS = (
    (1, 0), (3, 0), (1, 1), (3, 1), (2, 3), (2, 1), (2, 0), (3, 3),
    (2, 2), (3, 2), (1, 3), (1, 2), (0, 0), (0, 3), (0, 1), (0, 2),
)
FAR_FIRST = (2, 1, 3, 0)
O_ORDER = (3, 0, 1, 2)


def kernel(dims, x_hbm, wqkv_hbm, wout_hbm, y_ref,
           x_ext, w_kv, w_q, w_o, kv_all, kv_buf, q_all, q_t, q_relay,
           v_t, s_buf, m_cur, r_cur, m_run, l_run, acc, o_send, o_relay, o_all, y_acc,
           load_sem, x_sem, kv_send, kv_recv, q_send, q_recv, q_relay_sem,
           o_send_sem, o_recv, o_relay_sem):
    nx, ny, heads, kv_heads, head_dim = dims
    dev_tokens = x_hbm.shape[0]
    chip_tokens = 2 * dev_tokens
    row_keys = nx * chip_tokens
    kv_local = kv_heads // 2
    group = heads // kv_heads
    q_rows = group * head_dim
    feat = kv_local * q_rows
    rows = q_t.shape[2]
    tiles = rows // TILE
    main = LANES
    tail = chip_tokens - main
    cx, cy, core = lax.axis_index("cx"), lax.axis_index("cy"), lax.axis_index("core")
    other = 1 - core
    own_rows = pl.ds(pl.multiple_of(core * dev_tokens, 32), dev_tokens)
    other_rows = pl.ds(pl.multiple_of(other * dev_tokens, 32), dev_tokens)
    scale = head_dim ** -0.5 * math.log2(math.e)

    def head_at(dx):
        return lax.rem(cx + dx, nx)

    x_load = pltpu.make_async_copy(x_hbm, x_ext.at[own_rows], load_sem.at[0])
    x_load.start()
    kv_loads, q_loads = [], []
    for i, dx in enumerate(FAR_FIRST):
        for r in range(2):
            head = (core if r == 0 else other) * kv_local + head_at(dx)
            for part in range(2):
                src = pl.multiple_of((heads + part * kv_heads + head) * head_dim, head_dim)
                copy = pltpu.make_async_copy(
                    wqkv_hbm.at[pl.ds(src, head_dim)],
                    w_kv.at[pl.ds((4 * i + 2 * r + part) * head_dim, head_dim)],
                    load_sem.at[1 + 4 * i + 2 * r + part])
                copy.start()
                kv_loads.append(copy)
    for i, dx in enumerate(FAR_FIRST):
        src = pl.multiple_of(core * feat + head_at(dx) * q_rows, q_rows)
        copy = pltpu.make_async_copy(
            wqkv_hbm.at[pl.ds(src, q_rows)], w_q.at[pl.ds(i * q_rows, q_rows)], load_sem.at[1 + 4 * nx + i])
        copy.start()
        q_loads.append(copy)

    east = {"cx": lax.rem(cx + 1, nx)}
    west = {"cx": lax.rem(cx + nx - 1, nx)}
    north = {"cy": lax.rem(cy + 1, ny)}
    south = {"cy": lax.rem(cy + ny - 1, ny)}
    partner = {"core": other}
    across = {"cx": head_at(2)}
    by_dx = {0: {}, 1: east, 2: across, 3: west}
    targets = [partner, north, south]
    for dx in range(1, nx):
        targets += [by_dx[dx], {**by_dx[dx], **partner}]
    barrier = pltpu.get_barrier_semaphore()
    for target in targets:
        pl.semaphore_signal(barrier, inc=1, device_id=target, device_id_type=MESH)
    pl.semaphore_wait(barrier, len(targets))

    def remote(src, dst, send_sem, recv_sem, target):
        return pltpu.make_async_remote_copy(
            src_ref=src, dst_ref=dst, send_sem=send_sem, recv_sem=recv_sem, device_id=target, device_id_type=MESH)

    x_load.wait()
    x_copy = remote(x_ext.at[own_rows], x_ext.at[own_rows], x_sem.at[0], x_sem.at[1], partner)
    x_copy.start()
    q_t[:, head_dim:, :] = jnp.zeros((nx, LANES - head_dim, rows), jnp.bfloat16)
    acc[...] = jnp.zeros_like(acc)
    m_run[...] = jnp.full_like(m_run, -jnp.inf)
    l_run[...] = jnp.zeros_like(l_run)

    def kv_at(dx, dy):
        return dy * row_keys + dx * chip_tokens

    def kv_piece(dx, dy):
        return kv_buf.at[pl.ds(kv_at(dx, dy), chip_tokens)]

    def kv_half(dx, dy, r):
        return kv_buf.at[pl.ds(kv_at(dx, dy) + r * dev_tokens, dev_tokens)]

    def spread(src, dst_of, dx):
        remote(src, dst_of(3), kv_send.at[0], kv_recv.at[3, dx], north).start()
        remote(src, dst_of(1), kv_send.at[0], kv_recv.at[1, dx], south).start()

    for i in range(0, nx, 2):
        for copy in kv_loads[4 * i:4 * i + 8]:
            copy.wait()
        part = lax.dot_general(
            x_ext[own_rows], w_kv[4 * i * head_dim:(4 * i + 8) * head_dim], NT, preferred_element_type=jnp.float32)
        for k in range(4):
            kv_all[2 * i + k] = part[:, k * LANES:(k + 1) * LANES].astype(jnp.bfloat16)
        for k in range(4):
            dx, r = FAR_FIRST[i + k // 2], k % 2
            src = kv_all.at[2 * i + k]
            back = (nx - dx) % nx
            if dx:
                target = {**by_dx[dx], **partner} if r else by_dx[dx]
                remote(src, kv_half(back, 0, r), kv_send.at[0], kv_recv.at[0, back], target).start()
            elif r:
                remote(src, kv_half(0, 0, 1), kv_send.at[1], kv_recv.at[0, 0], partner).start()
            else:
                spread(src, lambda dy: kv_half(0, dy, 0), 0)
                kv_buf[kv_at(0, 0):kv_at(0, 0) + dev_tokens] = kv_all[2 * i + k]
    o_load = pltpu.make_async_copy(wout_hbm, w_o, load_sem.at[1 + 5 * nx])
    o_load.start()

    x_copy.wait()
    x_ext[chip_tokens:chip_tokens + tail] = x_ext[main:chip_tokens]
    lane = lax.broadcasted_iota(jnp.int32, (head_dim, LANES), 1)
    half_dim = head_dim // 2
    for i in range(0, nx, 2):
        results = []
        for k in (i, i + 1):
            q_loads[k].wait()
        for k in (i, i + 1):
            results.append(lax.dot_general(
                w_q[k * q_rows:(k + 1) * q_rows], x_ext[...], NT, preferred_element_type=jnp.float32))
        for k, res in zip((i, i + 1), results):
            dst = q_all.at[FAR_FIRST[k]] if FAR_FIRST[k] else q_t.at[0, pl.ds(0, head_dim)]
            for g in range(group):
                dst[:, g * LANES:(g + 1) * LANES] = res[g * head_dim:(g + 1) * head_dim, :main].astype(jnp.bfloat16)
            for pair in range(group // 2):
                lo = res[2 * pair * head_dim:(2 * pair + 1) * head_dim, main:]
                hi = res[(2 * pair + 1) * head_dim:(2 * pair + 2) * head_dim, main:]
                dst[:, (group + pair) * LANES:(group + pair + 1) * LANES] = (
                    jnp.where(lane < tail, lo, hi).astype(jnp.bfloat16))
        for k in (i, i + 1):
            dx = FAR_FIRST[k]
            if dx == 2:
                for half, target in ((0, east), (1, west)):
                    remote(q_all.at[2, pl.ds(half * half_dim, half_dim)], q_relay.at[half],
                           q_send, q_relay_sem.at[half], target).start()
            elif dx:
                remote(q_all.at[dx], q_t.at[nx - dx, pl.ds(0, head_dim)],
                       q_send, q_recv.at[nx - dx], by_dx[dx]).start()

    def arrive(ref, sem):
        remote(ref, ref, q_send, sem, partner).wait_recv()

    def kv_row(dx):
        if dx:
            arrive(kv_piece(dx, 0), kv_recv.at[0, dx])
            spread(kv_piece(dx, 0), lambda dy: kv_piece(dx, dy), dx)
        else:
            arrive(kv_half(0, 0, 1), kv_recv.at[0, 0])
            spread(kv_half(0, 0, 1), lambda dy: kv_half(0, dy, 1), 0)

    def kv_side(dx, dy):
        arrive(kv_piece(dx, dy), kv_recv.at[dy, dx])
        if dy == 3 and dx % 2 == 0:
            remote(kv_piece(dx, 3), kv_piece(dx, 2), kv_send.at[0], kv_recv.at[2, dx], north).start()
        if dy == 1 and dx % 2 == 1:
            remote(kv_piece(dx, 1), kv_piece(dx, 2), kv_send.at[0], kv_recv.at[2, dx], south).start()

    def q_relay_on():
        for half, target in ((0, east), (1, west)):
            arrive(q_relay.at[half], q_relay_sem.at[half])
            remote(q_relay.at[half], q_t.at[2, pl.ds(half * half_dim, half_dim)],
                   q_send, q_recv.at[2], target).start()

    def q_arrive(dx):
        arrive(q_t.at[dx, pl.ds(0, head_dim)], q_recv.at[dx])

    def o_relay_on():
        for half, target in ((0, east), (1, {**west, **partner})):
            arrive(o_relay.at[half], o_relay_sem.at[half])
            remote(o_relay.at[half], o_all.at[half, 2], o_send_sem.at[0], o_recv.at[half, 2], target).start()

    def keys(dy):
        return kv_buf[kv_at(0, dy):kv_at(0, dy) + row_keys]

    def score(q, dy, t):
        cols = slice(t * TILE, (t + 1) * TILE)
        scores = jnp.dot(keys(dy), q_t[q, :, cols], preferred_element_type=jnp.float32)
        old_max = m_run[q, :, cols]
        new_max = jnp.maximum(old_max, jnp.max(scores, axis=0, keepdims=True))
        m_run[q, :, cols] = new_max
        m_cur[:, cols] = new_max
        r_cur[:, cols] = jnp.exp2((old_max - new_max) * scale)
        s_buf[t] = scores

    def absorb(q, dy, t):
        cols = slice(t * TILE, (t + 1) * TILE)
        rescale = r_cur[:, cols]
        weights = jnp.exp2((s_buf[t] - m_cur[:, cols]) * scale)
        l_run[q, :, cols] = l_run[q, :, cols] * rescale + jnp.sum(weights, axis=0, keepdims=True)
        acc[q, :, cols] = acc[q, :, cols] * rescale + jnp.dot(
            v_t[dy], weights.astype(jnp.bfloat16), preferred_element_type=jnp.float32)

    def finish(q):
        out = acc[q] / l_run[q]
        dst = o_send.at[q]
        for pair in range(group // 2):
            cols = slice(pair * LANES, (pair + 1) * LANES)
            first = 2 * pair * LANES
            both = jnp.concatenate([out[:, first:first + LANES], out[:, first + LANES:first + 2 * LANES]], axis=0)
            dst[:main, cols] = jnp.transpose(both, (1, 0)).astype(jnp.bfloat16)
            ends = out[:, (group + pair) * LANES:(group + pair + 1) * LANES]
            both = jnp.concatenate([ends, pltpu.roll(ends, tail, 1)], axis=0)
            dst[main:, cols] = jnp.transpose(both, (1, 0))[:tail].astype(jnp.bfloat16)
        mine, theirs = o_send.at[q, own_rows], o_send.at[q, other_rows]
        if q == 2:
            remote(mine, o_relay.at[0], o_send_sem.at[0], o_relay_sem.at[0], east).start()
            remote(theirs, o_relay.at[1], o_send_sem.at[0], o_relay_sem.at[1], west).start()
        elif q:
            target = east if q == 1 else west
            remote(mine, o_all.at[0, nx - q], o_send_sem.at[0], o_recv.at[0, nx - q], target).start()
            remote(theirs, o_all.at[1, nx - q], o_send_sem.at[0], o_recv.at[1, nx - q], {**target, **partner}).start()
        else:
            remote(theirs, o_all.at[1, 0], o_send_sem.at[1], o_recv.at[1, 0], partner).start()
            o_all[0, 0] = o_send[0, own_rows]

    events = {n: [] for n in range(len(STEPS) + 1)}
    def row(*dxs):
        return [functools.partial(kv_row, dx) for dx in dxs]

    def side(*pieces):
        return [functools.partial(kv_side, dx, dy) for dx, dy in pieces]

    def query(dx):
        return [functools.partial(q_arrive, dx)]

    events[0] = row(0, 1, 2, 3) + [q_relay_on] + query(1)
    events[1] = side((0, 1), (1, 1)) + query(3) + side((1, 3), (2, 3))
    events[2] = side((0, 3), (2, 1), (3, 1))
    events[4] = query(2) + side((3, 3))
    events[5] = side((1, 2))
    events[8] = side((3, 2), (2, 2), (0, 2))
    events[15] = [o_relay_on]
    last_of = {q: max(n for n, s in enumerate(STEPS) if s[0] == q) for q in range(nx)}
    first_of = {dy: min(n for n, s in enumerate(STEPS) if s[1] == dy) for dy in range(ny)}

    for n in range(len(STEPS) + 1):
        for event in events[n]:
            event()
        if n < len(STEPS) and first_of[STEPS[n][1]] == n:
            dy = STEPS[n][1]
            v_t[dy] = jnp.transpose(keys(dy).astype(jnp.float32), (1, 0))[head_dim:].astype(jnp.bfloat16)
        for t in range(tiles):
            if n:
                absorb(*STEPS[n - 1], t)
            if n < len(STEPS):
                score(*STEPS[n], t)
        if n and last_of[STEPS[n - 1][0]] == n - 1:
            finish(STEPS[n - 1][0])

    o_load.wait()
    for i, dx in enumerate(O_ORDER):
        total = None
        for r in range(2):
            if dx or r:
                arrive(o_all.at[r, dx], o_recv.at[r, dx])
            first = ((core if r == 0 else other) * kv_local + head_at(dx)) * q_rows
            term = jnp.dot(o_all[r, dx], w_o[pl.ds(pl.multiple_of(first, q_rows), q_rows)],
                           preferred_element_type=jnp.float32)
            total = term if total is None else total + term
        if i == 0:
            y_acc[...] = total
        elif i < nx - 1:
            y_acc[...] += total
        else:
            y_ref[...] = (y_acc[...] + total).astype(jnp.bfloat16)

    for ref, sem in ((kv_buf.at[pl.ds(0, (nx * ny - 1) * chip_tokens)], kv_send.at[0]), (kv_all.at[0], kv_send.at[1]), (q_all, q_send), (o_all, o_send_sem.at[0]), (o_all.at[1, 0], o_send_sem.at[1])):
        remote(ref, ref, sem, x_sem.at[1], partner).wait_send()


def solution(mesh):
    nx, ny = mesh.shape["cx"], mesh.shape["cy"]
    seq_spec = P("dp", ("cy", "cx", "core"))

    def local_layer(x_loc, w_qkv, w_out):
        heads, head_dim, width = w_out.shape
        kv_heads = (w_qkv.shape[1] - heads) // 2
        tokens = x_loc.shape[1]
        kv_local = kv_heads // 2
        group = heads // kv_heads
        q_rows = group * head_dim
        feat = kv_local * q_rows
        rows = group * 2 * tokens
        dims = (nx, ny, heads, kv_heads, head_dim)
        w_rows = jnp.transpose(w_qkv, (1, 2, 0)).reshape(-1, width)
        hbm = pl.BlockSpec(memory_space=pl.ANY)
        half = jnp.bfloat16
        y = pl.pallas_call(
            functools.partial(kernel, dims),
            out_shape=jax.ShapeDtypeStruct((tokens, width), half),
            in_specs=[hbm] * 3,
            out_specs=pl.BlockSpec(memory_space=pltpu.VMEM),
            scratch_shapes=[
                pltpu.VMEM((TILE, width), half),
                pltpu.VMEM((2 * kv_heads * head_dim, width), half),
                pltpu.VMEM((feat, width), half),
                pltpu.VMEM((heads * head_dim, width), half),
                pltpu.VMEM((kv_heads, tokens, LANES), half),
                pltpu.VMEM((ny * nx * 2 * tokens, LANES), half),
                pltpu.VMEM((nx, head_dim, rows), half),
                pltpu.VMEM((nx, LANES, rows), half),
                pltpu.VMEM((2, head_dim // 2, rows), half),
                pltpu.VMEM((ny, head_dim, nx * 2 * tokens), half),
                pltpu.VMEM((rows // TILE, nx * 2 * tokens, TILE), jnp.float32),
                pltpu.VMEM((1, rows), jnp.float32),
                pltpu.VMEM((1, rows), jnp.float32),
                pltpu.VMEM((nx, 1, rows), jnp.float32),
                pltpu.VMEM((nx, 1, rows), jnp.float32),
                pltpu.VMEM((nx, head_dim, rows), jnp.float32),
                pltpu.VMEM((nx, 2 * tokens, q_rows), half),
                pltpu.VMEM((2, tokens, q_rows), half),
                pltpu.VMEM((2, nx, tokens, q_rows), half),
                pltpu.VMEM((tokens, width), jnp.float32),
                pltpu.SemaphoreType.DMA((2 + 5 * nx,)),
                pltpu.SemaphoreType.DMA((2,)),
                pltpu.SemaphoreType.DMA((2,)),
                pltpu.SemaphoreType.DMA((ny, nx)),
                pltpu.SemaphoreType.DMA,
                pltpu.SemaphoreType.DMA((nx,)),
                pltpu.SemaphoreType.DMA((2,)),
                pltpu.SemaphoreType.DMA((2,)),
                pltpu.SemaphoreType.DMA((2, nx)),
                pltpu.SemaphoreType.DMA((2,)),
            ],
            compiler_params=pltpu.CompilerParams(
                collective_id=0, has_side_effects=True, vmem_limit_bytes=54600 * 1024),
        )(x_loc[0], w_rows, w_out.reshape(heads * head_dim, width))
        return y[None]

    return jax.shard_map(local_layer, mesh=mesh, in_specs=(seq_spec, P(), P()), out_specs=seq_spec, check_vma=False)
```

time: 38.8 us -> 34.9 us (0.90)
  Pallas kernels: 36.9 us -> 34.1 us
  local copies, waits for them, and re-layouts: 1.74 us -> 0.75 us
    pallas_call x1, Pallas kernels: 36.9 us -> 34.1 us  [local_layer(): pl.pallas_call(functools.partial(kernel, dims), out_shape=jax.ShapeDtypeS...]
    unnamed x3 -> x1, local copies, waits for them, and re-layouts: 1.74 us -> 0.75 us
where the time goes in v5:
time: 34.9 us
  Pallas kernels  34.1 us (98%)
  local copies, waits for them, and re-layouts  0.75 us (2%)
    pallas_call x1, Pallas kernels, local_layer(): pl.pallas_call(functools.partial(kernel, dims), out_shape=jax.ShapeDtypeS...  34.1 us
    unnamed x1, local copies, waits for them, and re-layouts  0.75 us

profile of v5, /device:TPU:97, one launch (start us, length us, event | category | flops | bytes accessed | tf_op | source)
XLA Modules:
  0.0 34.9 jit_solution(18226662946451665698)
XLA Ops:
  0.0 34.1 %shard_map.37 = bf16[96,2048]{1,0:T(8,128)(2,1)S(1)} custom-call(bf16[96,2048]{1,0:T(8,128)(2,1)} %bitcast.9, bf16[3072,2048]{1,0:T(8,128)(2,1)} %bitcast.7, bf16[2048,2048]{1,0:T(8,128)(2,1)} %bitcast.8), custom_call_target="tpu_custom_call" | custom-call | tf_op jit(solution)/shard_map/pallas_call | solution.py:311
  34.1 0.7 %copy.5 = bf16[1,96,2048]{2,1,0:T(8,128)(2,1)} copy(bf16[1,96,2048]{2,1,0:T(8,128)(2,1)S(1)} %bitcast.6) | data formatting | bytes 786432

commit v6 on v5

--- a/solution.py
+++ b/solution.py
@@ -195,20 +195,20 @@
     def keys(dy):
         return kv_buf[kv_at(0, dy):kv_at(0, dy) + row_keys]
 
-    def score(q, dy, t):
+    def score(n, q, dy, t):
         cols = slice(t * TILE, (t + 1) * TILE)
         scores = jnp.dot(keys(dy), q_t[q, :, cols], preferred_element_type=jnp.float32)
         old_max = m_run[q, :, cols]
         new_max = jnp.maximum(old_max, jnp.max(scores, axis=0, keepdims=True))
         m_run[q, :, cols] = new_max
-        m_cur[:, cols] = new_max
-        r_cur[:, cols] = jnp.exp2((old_max - new_max) * scale)
-        s_buf[t] = scores
-
-    def absorb(q, dy, t):
+        m_cur[n % 2, :, cols] = new_max
+        r_cur[n % 2, :, cols] = jnp.exp2((old_max - new_max) * scale)
+        s_buf[n % 2, t] = scores
+
+    def absorb(n, q, dy, t):
         cols = slice(t * TILE, (t + 1) * TILE)
-        rescale = r_cur[:, cols]
-        weights = jnp.exp2((s_buf[t] - m_cur[:, cols]) * scale)
+        rescale = r_cur[n % 2, :, cols]
+        weights = jnp.exp2((s_buf[n % 2, t] - m_cur[n % 2, :, cols]) * scale)
         l_run[q, :, cols] = l_run[q, :, cols] * rescale + jnp.sum(weights, axis=0, keepdims=True)
         acc[q, :, cols] = acc[q, :, cols] * rescale + jnp.dot(
             v_t[dy], weights.astype(jnp.bfloat16), preferred_element_type=jnp.float32)
@@ -263,10 +263,10 @@
             dy = STEPS[n][1]
             v_t[dy] = jnp.transpose(keys(dy).astype(jnp.float32), (1, 0))[head_dim:].astype(jnp.bfloat16)
         for t in range(tiles):
+            if n < len(STEPS):
+                score(n, *STEPS[n], t)
             if n:
-                absorb(*STEPS[n - 1], t)
-            if n < len(STEPS):
-                score(*STEPS[n], t)
+                absorb(n - 1, *STEPS[n - 1], t)
         if n and last_of[STEPS[n - 1][0]] == n - 1:
             finish(STEPS[n - 1][0])
 
@@ -324,9 +324,9 @@
                 pltpu.VMEM((nx, LANES, rows), half),
                 pltpu.VMEM((2, head_dim // 2, rows), half),
                 pltpu.VMEM((ny, head_dim, nx * 2 * tokens), half),
-                pltpu.VMEM((rows // TILE, nx * 2 * tokens, TILE), jnp.float32),
-                pltpu.VMEM((1, rows), jnp.float32),
-                pltpu.VMEM((1, rows), jnp.float32),
+                pltpu.VMEM((2, rows // TILE, nx * 2 * tokens, TILE), jnp.float32),
+                pltpu.VMEM((2, 1, rows), jnp.float32),
+                pltpu.VMEM((2, 1, rows), jnp.float32),
                 pltpu.VMEM((nx, 1, rows), jnp.float32),
                 pltpu.VMEM((nx, 1, rows), jnp.float32),
                 pltpu.VMEM((nx, head_dim, rows), jnp.float32),

time: 34.9 us -> 33.6 us (0.963)
  Pallas kernels: 34.1 us -> 32.8 us
    pallas_call x1, Pallas kernels: 34.1 us -> 32.8 us  [local_layer(): pl.pallas_call(functools.partial(kernel, dims), out_shape=jax.ShapeDtypeS...]
where the time goes in v6:
time: 33.6 us; the launch traced here: 33.5 us
  Pallas kernels  32.8 us (98%)
  local copies, waits for them, and re-layouts  0.75 us (2%)
    pallas_call x1, Pallas kernels, local_layer(): pl.pallas_call(functools.partial(kernel, dims), out_shape=jax.ShapeDtypeS...  32.8 us
    unnamed x1, local copies, waits for them, and re-layouts  0.75 us

profile of v6, /device:TPU:97, one launch (start us, length us, event | category | flops | bytes accessed | tf_op | source)
XLA Modules:
  0.0 33.5 jit_solution(3520733640042812386)
XLA Ops:
  0.0 32.8 %shard_map.37 = bf16[96,2048]{1,0:T(8,128)(2,1)S(1)} custom-call(bf16[96,2048]{1,0:T(8,128)(2,1)} %bitcast.9, bf16[3072,2048]{1,0:T(8,128)(2,1)} %bitcast.7, bf16[2048,2048]{1,0:T(8,128)(2,1)} %bitcast.8), custom_call_target="tpu_custom_call" | custom-call | tf_op jit(solution)/shard_map/pallas_call | solution.py:311
  32.8 0.7 %copy.5 = bf16[1,96,2048]{2,1,0:T(8,128)(2,1)} copy(bf16[1,96,2048]{2,1,0:T(8,128)(2,1)S(1)} %bitcast.6) | data formatting | bytes 786432

commit v7 on v6

--- a/solution.py
+++ b/solution.py
@@ -23,9 +23,9 @@
 
 def kernel(dims, x_hbm, wqkv_hbm, wout_hbm, y_ref,
            x_ext, w_kv, w_q, w_o, kv_all, kv_buf, q_all, q_t, q_relay,
-           v_t, s_buf, m_cur, r_cur, m_run, l_run, acc, o_send, o_relay, o_all, y_acc,
+           v_t, s_buf, m_cur, r_cur, m_run, l_run, acc, o_send, o_all, y_acc,
            load_sem, x_sem, kv_send, kv_recv, q_send, q_recv, q_relay_sem,
-           o_send_sem, o_recv, o_relay_sem):
+           o_send_sem, o_recv):
     nx, ny, heads, kv_heads, head_dim = dims
     dev_tokens = x_hbm.shape[0]
     chip_tokens = 2 * dev_tokens
@@ -187,11 +187,6 @@
     def q_arrive(dx):
         arrive(q_t.at[dx, pl.ds(0, head_dim)], q_recv.at[dx])
 
-    def o_relay_on():
-        for half, target in ((0, east), (1, {**west, **partner})):
-            arrive(o_relay.at[half], o_relay_sem.at[half])
-            remote(o_relay.at[half], o_all.at[half, 2], o_send_sem.at[0], o_recv.at[half, 2], target).start()
-
     def keys(dy):
         return kv_buf[kv_at(0, dy):kv_at(0, dy) + row_keys]
 
@@ -225,11 +220,8 @@
             both = jnp.concatenate([ends, pltpu.roll(ends, tail, 1)], axis=0)
             dst[main:, cols] = jnp.transpose(both, (1, 0))[:tail].astype(jnp.bfloat16)
         mine, theirs = o_send.at[q, own_rows], o_send.at[q, other_rows]
-        if q == 2:
-            remote(mine, o_relay.at[0], o_send_sem.at[0], o_relay_sem.at[0], east).start()
-            remote(theirs, o_relay.at[1], o_send_sem.at[0], o_relay_sem.at[1], west).start()
-        elif q:
-            target = east if q == 1 else west
+        if q:
+            target = by_dx[q]
             remote(mine, o_all.at[0, nx - q], o_send_sem.at[0], o_recv.at[0, nx - q], target).start()
             remote(theirs, o_all.at[1, nx - q], o_send_sem.at[0], o_recv.at[1, nx - q], {**target, **partner}).start()
         else:
@@ -252,7 +244,6 @@
     events[4] = query(2) + side((3, 3))
     events[5] = side((1, 2))
     events[8] = side((3, 2), (2, 2), (0, 2))
-    events[15] = [o_relay_on]
     last_of = {q: max(n for n, s in enumerate(STEPS) if s[0] == q) for q in range(nx)}
     first_of = {dy: min(n for n, s in enumerate(STEPS) if s[1] == dy) for dy in range(ny)}
 
@@ -287,7 +278,7 @@
         else:
             y_ref[...] = (y_acc[...] + total).astype(jnp.bfloat16)
 
-    for ref, sem in ((kv_buf.at[pl.ds(0, (nx * ny - 1) * chip_tokens)], kv_send.at[0]), (kv_all.at[0], kv_send.at[1]), (q_all, q_send), (o_all, o_send_sem.at[0]), (o_all.at[1, 0], o_send_sem.at[1])):
+    for ref, sem in ((kv_buf.at[pl.ds(0, (nx * ny - 1) * chip_tokens)], kv_send.at[0]), (kv_all.at[0], kv_send.at[1]), (q_all, q_send), (o_all.at[:, pl.ds(0, nx - 1)], o_send_sem.at[0]), (o_all.at[1, 0], o_send_sem.at[1])):
         remote(ref, ref, sem, x_sem.at[1], partner).wait_send()
 
 
@@ -331,7 +322,6 @@
                 pltpu.VMEM((nx, 1, rows), jnp.float32),
                 pltpu.VMEM((nx, head_dim, rows), jnp.float32),
                 pltpu.VMEM((nx, 2 * tokens, q_rows), half),
-                pltpu.VMEM((2, tokens, q_rows), half),
                 pltpu.VMEM((2, nx, tokens, q_rows), half),
                 pltpu.VMEM((tokens, width), jnp.float32),
                 pltpu.SemaphoreType.DMA((2 + 5 * nx,)),
@@ -343,7 +333,6 @@
                 pltpu.SemaphoreType.DMA((2,)),
                 pltpu.SemaphoreType.DMA((2,)),
                 pltpu.SemaphoreType.DMA((2, nx)),
-                pltpu.SemaphoreType.DMA((2,)),
             ],
             compiler_params=pltpu.CompilerParams(
                 collective_id=0, has_side_effects=True, vmem_limit_bytes=54600 * 1024),

time: 33.6 us -> 33.3 us (level)
  no operation moved by 1% of the time
where the time goes in v7:
time: 33.3 us; the launch traced here: 33.2 us
  Pallas kernels  32.5 us (98%)
  local copies, waits for them, and re-layouts  0.75 us (2%)
    pallas_call x1, Pallas kernels, local_layer(): pl.pallas_call(functools.partial(kernel, dims), out_shape=jax.ShapeDtypeS...  32.5 us
    unnamed x1, local copies, waits for them, and re-layouts  0.75 us

profile of v7, /device:TPU:97, one launch (start us, length us, event | category | flops | bytes accessed | tf_op | source)
XLA Modules:
  0.0 33.2 jit_solution(10188142250310941799)
XLA Ops:
  0.0 32.5 %shard_map.37 = bf16[96,2048]{1,0:T(8,128)(2,1)S(1)} custom-call(bf16[96,2048]{1,0:T(8,128)(2,1)} %bitcast.9, bf16[3072,2048]{1,0:T(8,128)(2,1)} %bitcast.7, bf16[2048,2048]{1,0:T(8,128)(2,1)} %bitcast.8), custom_call_target="tpu_custom_call" | custom-call | tf_op jit(solution)/shard_map/pallas_call | solution.py:302
  32.5 0.7 %copy.5 = bf16[1,96,2048]{2,1,0:T(8,128)(2,1)} copy(bf16[1,96,2048]{2,1,0:T(8,128)(2,1)S(1)} %bitcast.6) | data formatting | bytes 786432

commit v8 on v7

--- a/solution.py
+++ b/solution.py
@@ -14,17 +14,18 @@
 NT = (((1,), (1,)), ((), ()))
 
 STEPS = (
-    (1, 0), (3, 0), (1, 1), (3, 1), (2, 3), (2, 1), (2, 0), (3, 3),
-    (2, 2), (3, 2), (1, 3), (1, 2), (0, 0), (0, 3), (0, 1), (0, 2),
+    (0, 0), (1, 0), (3, 0), (1, 1), (2, 3), (2, 0), (1, 3), (2, 1),
+    (2, 2), (3, 2), (1, 2), (3, 3), (3, 1), (0, 3), (0, 1), (0, 2),
 )
 FAR_FIRST = (2, 1, 3, 0)
+Q_ORDER = (1, 3, 2, 0)
 O_ORDER = (3, 0, 1, 2)
 
 
 def kernel(dims, x_hbm, wqkv_hbm, wout_hbm, y_ref,
-           x_ext, w_kv, w_q, w_o, kv_all, kv_buf, q_all, q_t, q_relay,
+           x_ext, w_kv, w_q, w_o, kv_all, kv_buf, q_all, q_t,
            v_t, s_buf, m_cur, r_cur, m_run, l_run, acc, o_send, o_all, y_acc,
-           load_sem, x_sem, kv_send, kv_recv, q_send, q_recv, q_relay_sem,
+           load_sem, x_sem, kv_send, kv_recv, q_send, q_recv,
            o_send_sem, o_recv):
     nx, ny, heads, kv_heads, head_dim = dims
     dev_tokens = x_hbm.shape[0]
@@ -61,7 +62,7 @@
                     load_sem.at[1 + 4 * i + 2 * r + part])
                 copy.start()
                 kv_loads.append(copy)
-    for i, dx in enumerate(FAR_FIRST):
+    for i, dx in enumerate(Q_ORDER):
         src = pl.multiple_of(core * feat + head_at(dx) * q_rows, q_rows)
         copy = pltpu.make_async_copy(
             wqkv_hbm.at[pl.ds(src, q_rows)], w_q.at[pl.ds(i * q_rows, q_rows)], load_sem.at[1 + 4 * nx + i])
@@ -133,7 +134,6 @@
     x_copy.wait()
     x_ext[chip_tokens:chip_tokens + tail] = x_ext[main:chip_tokens]
     lane = lax.broadcasted_iota(jnp.int32, (head_dim, LANES), 1)
-    half_dim = head_dim // 2
     for i in range(0, nx, 2):
         results = []
         for k in (i, i + 1):
@@ -142,7 +142,7 @@
             results.append(lax.dot_general(
                 w_q[k * q_rows:(k + 1) * q_rows], x_ext[...], NT, preferred_element_type=jnp.float32))
         for k, res in zip((i, i + 1), results):
-            dst = q_all.at[FAR_FIRST[k]] if FAR_FIRST[k] else q_t.at[0, pl.ds(0, head_dim)]
+            dst = q_all.at[Q_ORDER[k]] if Q_ORDER[k] else q_t.at[0, pl.ds(0, head_dim)]
             for g in range(group):
                 dst[:, g * LANES:(g + 1) * LANES] = res[g * head_dim:(g + 1) * head_dim, :main].astype(jnp.bfloat16)
             for pair in range(group // 2):
@@ -151,12 +151,8 @@
                 dst[:, (group + pair) * LANES:(group + pair + 1) * LANES] = (
                     jnp.where(lane < tail, lo, hi).astype(jnp.bfloat16))
         for k in (i, i + 1):
-            dx = FAR_FIRST[k]
-            if dx == 2:
-                for half, target in ((0, east), (1, west)):
-                    remote(q_all.at[2, pl.ds(half * half_dim, half_dim)], q_relay.at[half],
-                           q_send, q_relay_sem.at[half], target).start()
-            elif dx:
+            dx = Q_ORDER[k]
+            if dx:
                 remote(q_all.at[dx], q_t.at[nx - dx, pl.ds(0, head_dim)],
                        q_send, q_recv.at[nx - dx], by_dx[dx]).start()
 
@@ -177,12 +173,6 @@
             remote(kv_piece(dx, 3), kv_piece(dx, 2), kv_send.at[0], kv_recv.at[2, dx], north).start()
         if dy == 1 and dx % 2 == 1:
             remote(kv_piece(dx, 1), kv_piece(dx, 2), kv_send.at[0], kv_recv.at[2, dx], south).start()
-
-    def q_relay_on():
-        for half, target in ((0, east), (1, west)):
-            arrive(q_relay.at[half], q_relay_sem.at[half])
-            remote(q_relay.at[half], q_t.at[2, pl.ds(half * half_dim, half_dim)],
-                   q_send, q_recv.at[2], target).start()
 
     def q_arrive(dx):
         arrive(q_t.at[dx, pl.ds(0, head_dim)], q_recv.at[dx])
@@ -238,12 +228,12 @@
     def query(dx):
         return [functools.partial(q_arrive, dx)]
 
-    events[0] = row(0, 1, 2, 3) + [q_relay_on] + query(1)
-    events[1] = side((0, 1), (1, 1)) + query(3) + side((1, 3), (2, 3))
-    events[2] = side((0, 3), (2, 1), (3, 1))
-    events[4] = query(2) + side((3, 3))
-    events[5] = side((1, 2))
-    events[8] = side((3, 2), (2, 2), (0, 2))
+    events[0] = row(0, 2, 1, 3)
+    events[1] = side((0, 1)) + query(1)
+    events[2] = side((2, 3)) + query(3)
+    events[3] = side((1, 1), (2, 1), (0, 3), (3, 1))
+    events[4] = side((3, 3), (1, 3)) + query(2)
+    events[8] = side((0, 2), (1, 2), (2, 2), (3, 2))
     last_of = {q: max(n for n, s in enumerate(STEPS) if s[0] == q) for q in range(nx)}
     first_of = {dy: min(n for n, s in enumerate(STEPS) if s[1] == dy) for dy in range(ny)}
 
@@ -278,7 +268,7 @@
         else:
             y_ref[...] = (y_acc[...] + total).astype(jnp.bfloat16)
 
-    for ref, sem in ((kv_buf.at[pl.ds(0, (nx * ny - 1) * chip_tokens)], kv_send.at[0]), (kv_all.at[0], kv_send.at[1]), (q_all, q_send), (o_all.at[:, pl.ds(0, nx - 1)], o_send_sem.at[0]), (o_all.at[1, 0], o_send_sem.at[1])):
+    for ref, sem in ((kv_buf.at[pl.ds(0, (nx * ny - 1) * chip_tokens)], kv_send.at[0]), (kv_all.at[0], kv_send.at[1]), (q_all.at[pl.ds(0, nx - 1)], q_send), (o_all.at[:, pl.ds(0, nx - 1)], o_send_sem.at[0]), (o_all.at[1, 0], o_send_sem.at[1])):
         remote(ref, ref, sem, x_sem.at[1], partner).wait_send()
 
 
@@ -313,7 +303,6 @@
                 pltpu.VMEM((ny * nx * 2 * tokens, LANES), half),
                 pltpu.VMEM((nx, head_dim, rows), half),
                 pltpu.VMEM((nx, LANES, rows), half),
-                pltpu.VMEM((2, head_dim // 2, rows), half),
                 pltpu.VMEM((ny, head_dim, nx * 2 * tokens), half),
                 pltpu.VMEM((2, rows // TILE, nx * 2 * tokens, TILE), jnp.float32),
                 pltpu.VMEM((2, 1, rows), jnp.float32),
@@ -331,7 +320,6 @@
                 pltpu.SemaphoreType.DMA,
                 pltpu.SemaphoreType.DMA((nx,)),
                 pltpu.SemaphoreType.DMA((2,)),
-                pltpu.SemaphoreType.DMA((2,)),
                 pltpu.SemaphoreType.DMA((2, nx)),
             ],
             compiler_params=pltpu.CompilerParams(

time: 33.3 us -> 31.2 us (0.937)
  Pallas kernels: 32.5 us -> 30.4 us
    pallas_call x1, Pallas kernels: 32.5 us -> 30.4 us  [local_layer(): pl.pallas_call(functools.partial(kernel, dims), out_shape=jax.ShapeDtypeS...]
where the time goes in v8:
time: 31.2 us
  Pallas kernels  30.4 us (97%)
  local copies, waits for them, and re-layouts  0.75 us (2%)
    pallas_call x1, Pallas kernels, local_layer(): pl.pallas_call(functools.partial(kernel, dims), out_shape=jax.ShapeDtypeS...  30.4 us
    unnamed x1, local copies, waits for them, and re-layouts  0.75 us

profile of v8, /device:TPU:97, one launch (start us, length us, event | category | flops | bytes accessed | tf_op | source)
XLA Modules:
  0.0 31.2 jit_solution(4517758501149246650)
XLA Ops:
  0.0 30.4 %shard_map.37 = bf16[96,2048]{1,0:T(8,128)(2,1)S(1)} custom-call(bf16[96,2048]{1,0:T(8,128)(2,1)} %bitcast.9, bf16[3072,2048]{1,0:T(8,128)(2,1)} %bitcast.7, bf16[2048,2048]{1,0:T(8,128)(2,1)} %bitcast.8), custom_call_target="tpu_custom_call" | custom-call | tf_op jit(solution)/shard_map/pallas_call | solution.py:292
  30.4 0.7 %copy.5 = bf16[1,96,2048]{2,1,0:T(8,128)(2,1)} copy(bf16[1,96,2048]{2,1,0:T(8,128)(2,1)S(1)} %bitcast.6) | data formatting | bytes 786432

commit v9 on v8

--- a/solution.py
+++ b/solution.py
@@ -66,7 +66,6 @@
         src = pl.multiple_of(core * feat + head_at(dx) * q_rows, q_rows)
         copy = pltpu.make_async_copy(
             wqkv_hbm.at[pl.ds(src, q_rows)], w_q.at[pl.ds(i * q_rows, q_rows)], load_sem.at[1 + 4 * nx + i])
-        copy.start()
         q_loads.append(copy)
 
     east = {"cx": lax.rem(cx + 1, nx)}
@@ -112,6 +111,8 @@
     for i in range(0, nx, 2):
         for copy in kv_loads[4 * i:4 * i + 8]:
             copy.wait()
+        for copy in q_loads[i:i + 2]:
+            copy.start()
         part = lax.dot_general(
             x_ext[own_rows], w_kv[4 * i * head_dim:(4 * i + 8) * head_dim], NT, preferred_element_type=jnp.float32)
         for k in range(4):

time: 31.2 us -> 31.2 us (level)
  no operation moved by 1% of the time
where the time goes in v9:
time: 31.2 us
  Pallas kernels  30.4 us (97%)
  local copies, waits for them, and re-layouts  0.75 us (2%)
    pallas_call x1, Pallas kernels, local_layer(): pl.pallas_call(functools.partial(kernel, dims), out_shape=jax.ShapeDtypeS...  30.4 us
    unnamed x1, local copies, waits for them, and re-layouts  0.75 us

profile of v9, /device:TPU:97, one launch (start us, length us, event | category | flops | bytes accessed | tf_op | source)
XLA Modules:
  0.0 31.2 jit_solution(11194868227516818397)
XLA Ops:
  0.0 30.4 %shard_map.37 = bf16[96,2048]{1,0:T(8,128)(2,1)S(1)} custom-call(bf16[96,2048]{1,0:T(8,128)(2,1)} %bitcast.9, bf16[3072,2048]{1,0:T(8,128)(2,1)} %bitcast.7, bf16[2048,2048]{1,0:T(8,128)(2,1)} %bitcast.8), custom_call_target="tpu_custom_call" | custom-call | tf_op jit(solution)/shard_map/pallas_call | solution.py:293
  30.4 0.7 %copy.5 = bf16[1,96,2048]{2,1,0:T(8,128)(2,1)} copy(bf16[1,96,2048]{2,1,0:T(8,128)(2,1)S(1)} %bitcast.6) | data formatting | bytes 786432

commit v10 on v8

--- a/solution.py
+++ b/solution.py
@@ -17,13 +17,15 @@
     (0, 0), (1, 0), (3, 0), (1, 1), (2, 3), (2, 0), (1, 3), (2, 1),
     (2, 2), (3, 2), (1, 2), (3, 3), (3, 1), (0, 3), (0, 1), (0, 2),
 )
+SLOTS = (("s", 0), ("a", 0), ("s", 1), ("a", 1), ("s", 2), ("a", 2))
+END_SLOTS = (("s", 0), ("a", 0), ("a", 1), ("a", 2), ("s", 1), ("s", 2))
 FAR_FIRST = (2, 1, 3, 0)
 Q_ORDER = (1, 3, 2, 0)
 O_ORDER = (3, 0, 1, 2)
 
 
 def kernel(dims, x_hbm, wqkv_hbm, wout_hbm, y_ref,
-           x_ext, w_kv, w_q, w_o, kv_all, kv_buf, q_all, q_t,
+           x_ext, w_kv, w_q, w_o, kv_all, kv_buf, q_all, q_t, q_wide, k_wide,
            v_t, s_buf, m_cur, r_cur, m_run, l_run, acc, o_send, o_all, y_acc,
            load_sem, x_sem, kv_send, kv_recv, q_send, q_recv,
            o_send_sem, o_recv):
@@ -91,7 +93,7 @@
     x_load.wait()
     x_copy = remote(x_ext.at[own_rows], x_ext.at[own_rows], x_sem.at[0], x_sem.at[1], partner)
     x_copy.start()
-    q_t[:, head_dim:, :] = jnp.zeros((nx, LANES - head_dim, rows), jnp.bfloat16)
+    q_wide[:, head_dim:LANES, :] = jnp.zeros((nx, LANES - head_dim, rows), jnp.bfloat16)
     acc[...] = jnp.zeros_like(acc)
     m_run[...] = jnp.full_like(m_run, -jnp.inf)
     l_run[...] = jnp.zeros_like(l_run)
@@ -142,7 +144,7 @@
             results.append(lax.dot_general(
                 w_q[k * q_rows:(k + 1) * q_rows], x_ext[...], NT, preferred_element_type=jnp.float32))
         for k, res in zip((i, i + 1), results):
-            dst = q_all.at[Q_ORDER[k]] if Q_ORDER[k] else q_t.at[0, pl.ds(0, head_dim)]
+            dst = q_all.at[Q_ORDER[k]] if Q_ORDER[k] else q_t.at[0]
             for g in range(group):
                 dst[:, g * LANES:(g + 1) * LANES] = res[g * head_dim:(g + 1) * head_dim, :main].astype(jnp.bfloat16)
             for pair in range(group // 2):
@@ -153,7 +155,7 @@
         for k in (i, i + 1):
             dx = Q_ORDER[k]
             if dx:
-                remote(q_all.at[dx], q_t.at[nx - dx, pl.ds(0, head_dim)],
+                remote(q_all.at[dx], q_t.at[nx - dx],
                        q_send, q_recv.at[nx - dx], by_dx[dx]).start()
 
     def arrive(ref, sem):
@@ -175,25 +177,41 @@
             remote(kv_piece(dx, 1), kv_piece(dx, 2), kv_send.at[0], kv_recv.at[2, dx], south).start()
 
     def q_arrive(dx):
-        arrive(q_t.at[dx, pl.ds(0, head_dim)], q_recv.at[dx])
-
-    def keys(dy):
-        return kv_buf[kv_at(0, dy):kv_at(0, dy) + row_keys]
+        arrive(q_t.at[dx], q_recv.at[dx])
+
+    def widen_queries(q):
+        scaled = q_t[q].astype(jnp.float32) * scale
+        high = scaled.astype(jnp.bfloat16)
+        rest = scaled - high.astype(jnp.float32)
+        middle = rest.astype(jnp.bfloat16)
+        low = (rest - middle.astype(jnp.float32)).astype(jnp.bfloat16)
+        q_wide[q, :head_dim] = high
+        q_wide[q, LANES:LANES + head_dim] = middle
+        q_wide[q, LANES + head_dim:] = low
+
+    def widen_keys(dy):
+        pair = kv_buf[kv_at(0, dy):kv_at(0, dy) + row_keys]
+        wide = pair.astype(jnp.float32)
+        first = lax.broadcasted_iota(jnp.int32, wide.shape, 1) < head_dim
+        twice = jnp.where(first, wide, pltpu.roll(wide, head_dim, 1))
+        k_wide[dy, :, :LANES] = pair
+        k_wide[dy, :, LANES:] = twice.astype(jnp.bfloat16)
+        v_t[dy] = jnp.transpose(wide, (1, 0))[head_dim:].astype(jnp.bfloat16)
 
     def score(n, q, dy, t):
         cols = slice(t * TILE, (t + 1) * TILE)
-        scores = jnp.dot(keys(dy), q_t[q, :, cols], preferred_element_type=jnp.float32)
+        scores = jnp.dot(k_wide[dy], q_wide[q, :, cols], preferred_element_type=jnp.float32)
         old_max = m_run[q, :, cols]
         new_max = jnp.maximum(old_max, jnp.max(scores, axis=0, keepdims=True))
         m_run[q, :, cols] = new_max
         m_cur[n % 2, :, cols] = new_max
-        r_cur[n % 2, :, cols] = jnp.exp2((old_max - new_max) * scale)
+        r_cur[n % 2, :, cols] = jnp.exp2(old_max - new_max)
         s_buf[n % 2, t] = scores
 
     def absorb(n, q, dy, t):
         cols = slice(t * TILE, (t + 1) * TILE)
         rescale = r_cur[n % 2, :, cols]
-        weights = jnp.exp2((s_buf[n % 2, t] - m_cur[n % 2, :, cols]) * scale)
+        weights = jnp.exp2(s_buf[n % 2, t] - m_cur[n % 2, :, cols])
         l_run[q, :, cols] = l_run[q, :, cols] * rescale + jnp.sum(weights, axis=0, keepdims=True)
         acc[q, :, cols] = acc[q, :, cols] * rescale + jnp.dot(
             v_t[dy], weights.astype(jnp.bfloat16), preferred_element_type=jnp.float32)
@@ -235,6 +253,7 @@
     events[4] = side((3, 3), (1, 3)) + query(2)
     events[8] = side((0, 2), (1, 2), (2, 2), (3, 2))
     last_of = {q: max(n for n, s in enumerate(STEPS) if s[0] == q) for q in range(nx)}
+    first_use = {q: min(n for n, s in enumerate(STEPS) if s[0] == q) for q in range(nx)}
     first_of = {dy: min(n for n, s in enumerate(STEPS) if s[1] == dy) for dy in range(ny)}
 
     for n in range(len(STEPS) + 1):
@@ -242,13 +261,16 @@
             event()
         if n < len(STEPS) and first_of[STEPS[n][1]] == n:
             dy = STEPS[n][1]
-            v_t[dy] = jnp.transpose(keys(dy).astype(jnp.float32), (1, 0))[head_dim:].astype(jnp.bfloat16)
-        for t in range(tiles):
-            if n < len(STEPS):
+            widen_keys(dy)
+        if n < len(STEPS) and first_use[STEPS[n][0]] == n:
+            widen_queries(STEPS[n][0])
+        ends = n and last_of[STEPS[n - 1][0]] == n - 1
+        for work, t in (END_SLOTS if ends else SLOTS):
+            if work == "s" and n < len(STEPS):
                 score(n, *STEPS[n], t)
-            if n:
+            if work == "a" and n:
                 absorb(n - 1, *STEPS[n - 1], t)
-        if n and last_of[STEPS[n - 1][0]] == n - 1:
+        if ends:
             finish(STEPS[n - 1][0])
 
     o_load.wait()
@@ -302,7 +324,9 @@
                 pltpu.VMEM((kv_heads, tokens, LANES), half),
                 pltpu.VMEM((ny * nx * 2 * tokens, LANES), half),
                 pltpu.VMEM((nx, head_dim, rows), half),
-                pltpu.VMEM((nx, LANES, rows), half),
+                pltpu.VMEM((nx, head_dim, rows), half),
+                pltpu.VMEM((nx, 2 * LANES, rows), half),
+                pltpu.VMEM((ny, nx * 2 * tokens, 2 * LANES), half),
                 pltpu.VMEM((ny, head_dim, nx * 2 * tokens), half),
                 pltpu.VMEM((2, rows // TILE, nx * 2 * tokens, TILE), jnp.float32),
                 pltpu.VMEM((2, 1, rows), jnp.float32),

time: 31.2 us -> 31.4 us (level)
  no operation moved by 1% of the time
where the time goes in v10:
time: 31.4 us; the launch traced here: 31.3 us
  Pallas kernels  30.6 us (97%)
  local copies, waits for them, and re-layouts  0.75 us (2%)
    pallas_call x1, Pallas kernels, local_layer(): pl.pallas_call(functools.partial(kernel, dims), out_shape=jax.ShapeDtypeS...  30.6 us
    unnamed x1, local copies, waits for them, and re-layouts  0.75 us

profile of v10, /device:TPU:97, one launch (start us, length us, event | category | flops | bytes accessed | tf_op | source)
XLA Modules:
  0.0 31.3 jit_solution(17472276928166512025)
XLA Ops:
  0.0 30.6 %shard_map.37 = bf16[96,2048]{1,0:T(8,128)(2,1)S(1)} custom-call(bf16[96,2048]{1,0:T(8,128)(2,1)} %bitcast.9, bf16[3072,2048]{1,0:T(8,128)(2,1)} %bitcast.7, bf16[2048,2048]{1,0:T(8,128)(2,1)} %bitcast.8), custom_call_target="tpu_custom_call" | custom-call | tf_op jit(solution)/shard_map/pallas_call | solution.py:314
  30.6 0.7 %copy.5 = bf16[1,96,2048]{2,1,0:T(8,128)(2,1)} copy(bf16[1,96,2048]{2,1,0:T(8,128)(2,1)S(1)} %bitcast.6) | data formatting | bytes 786432

commit v11 on v8

--- a/solution.py
+++ b/solution.py
@@ -17,9 +17,11 @@
     (0, 0), (1, 0), (3, 0), (1, 1), (2, 3), (2, 0), (1, 3), (2, 1),
     (2, 2), (3, 2), (1, 2), (3, 3), (3, 1), (0, 3), (0, 1), (0, 2),
 )
+SLOTS = (("s", 0), ("a", 0), ("s", 1), ("a", 1), ("s", 2), ("a", 2))
+END_SLOTS = (("s", 0), ("a", 0), ("a", 1), ("s", 1), ("a", 2), ("s", 2))
 FAR_FIRST = (2, 1, 3, 0)
 Q_ORDER = (1, 3, 2, 0)
-O_ORDER = (3, 0, 1, 2)
+O_ORDER = (2, 0, 3, 1)
 
 
 def kernel(dims, x_hbm, wqkv_hbm, wout_hbm, y_ref,
@@ -243,16 +245,20 @@
         if n < len(STEPS) and first_of[STEPS[n][1]] == n:
             dy = STEPS[n][1]
             v_t[dy] = jnp.transpose(keys(dy).astype(jnp.float32), (1, 0))[head_dim:].astype(jnp.bfloat16)
-        for t in range(tiles):
-            if n < len(STEPS):
+        ends = n and last_of[STEPS[n - 1][0]] == n - 1
+        for work, t in (END_SLOTS if ends else SLOTS):
+            if work == "s" and n < len(STEPS):
                 score(n, *STEPS[n], t)
-            if n:
+            if work == "a" and n:
                 absorb(n - 1, *STEPS[n - 1], t)
-        if n and last_of[STEPS[n - 1][0]] == n - 1:
+        if ends:
             finish(STEPS[n - 1][0])
 
     o_load.wait()
     for i, dx in enumerate(O_ORDER):
+        if i == nx - 1:
+            for ref, sem in ((kv_buf.at[pl.ds(0, (nx * ny - 1) * chip_tokens)], kv_send.at[0]), (kv_all.at[0], kv_send.at[1]), (q_all.at[pl.ds(0, nx - 1)], q_send), (o_all.at[:, pl.ds(0, nx - 1)], o_send_sem.at[0]), (o_all.at[1, 0], o_send_sem.at[1])):
+                remote(ref, ref, sem, x_sem.at[1], partner).wait_send()
         total = None
         for r in range(2):
             if dx or r:
@@ -267,9 +273,6 @@
             y_acc[...] += total
         else:
             y_ref[...] = (y_acc[...] + total).astype(jnp.bfloat16)
-
-    for ref, sem in ((kv_buf.at[pl.ds(0, (nx * ny - 1) * chip_tokens)], kv_send.at[0]), (kv_all.at[0], kv_send.at[1]), (q_all.at[pl.ds(0, nx - 1)], q_send), (o_all.at[:, pl.ds(0, nx - 1)], o_send_sem.at[0]), (o_all.at[1, 0], o_send_sem.at[1])):
-        remote(ref, ref, sem, x_sem.at[1], partner).wait_send()
 
 
 def solution(mesh):

time: 31.2 us -> 30.3 us (0.971)
  Pallas kernels: 30.4 us -> 29.5 us
    pallas_call x1, Pallas kernels: 30.4 us -> 29.5 us  [local_layer(): pl.pallas_call(functools.partial(kernel, dims), out_shape=jax.ShapeDtypeS...]
where the time goes in v11:
time: 30.3 us
  Pallas kernels  29.5 us (97%)
  local copies, waits for them, and re-layouts  0.75 us (2%)
    pallas_call x1, Pallas kernels, local_layer(): pl.pallas_call(functools.partial(kernel, dims), out_shape=jax.ShapeDtypeS...  29.5 us
    unnamed x1, local copies, waits for them, and re-layouts  0.75 us

profile of v11, /device:TPU:97, one launch (start us, length us, event | category | flops | bytes accessed | tf_op | source)
XLA Modules:
  0.0 30.3 jit_solution(12513164272705759840)
XLA Ops:
  0.0 29.5 %shard_map.37 = bf16[96,2048]{1,0:T(8,128)(2,1)S(1)} custom-call(bf16[96,2048]{1,0:T(8,128)(2,1)} %bitcast.9, bf16[3072,2048]{1,0:T(8,128)(2,1)} %bitcast.7, bf16[2048,2048]{1,0:T(8,128)(2,1)} %bitcast.8), custom_call_target="tpu_custom_call" | custom-call | tf_op jit(solution)/shard_map/pallas_call | solution.py:295
  29.5 0.7 %copy.5 = bf16[1,96,2048]{2,1,0:T(8,128)(2,1)} copy(bf16[1,96,2048]{2,1,0:T(8,128)(2,1)S(1)} %bitcast.6) | data formatting | bytes 786432

commit v12 on v11

--- a/solution.py
+++ b/solution.py
@@ -14,8 +14,8 @@
 NT = (((1,), (1,)), ((), ()))
 
 STEPS = (
-    (0, 0), (1, 0), (3, 0), (1, 1), (2, 3), (2, 0), (1, 3), (2, 1),
-    (2, 2), (3, 2), (1, 2), (3, 3), (3, 1), (0, 3), (0, 1), (0, 2),
+    (0, 0), (3, 0), (1, 0), (2, 1), (3, 1), (2, 3), (3, 3), (1, 1),
+    (2, 0), (2, 2), (1, 3), (3, 2), (1, 2), (0, 3), (0, 2), (0, 1),
 )
 SLOTS = (("s", 0), ("a", 0), ("s", 1), ("a", 1), ("s", 2), ("a", 2))
 END_SLOTS = (("s", 0), ("a", 0), ("a", 1), ("s", 1), ("a", 2), ("s", 2))
@@ -230,12 +230,12 @@
     def query(dx):
         return [functools.partial(q_arrive, dx)]
 
-    events[0] = row(0, 2, 1, 3)
-    events[1] = side((0, 1)) + query(1)
-    events[2] = side((2, 3)) + query(3)
-    events[3] = side((1, 1), (2, 1), (0, 3), (3, 1))
-    events[4] = side((3, 3), (1, 3)) + query(2)
-    events[8] = side((0, 2), (1, 2), (2, 2), (3, 2))
+    events[0] = row(0, 2, 1, 3) + side((0, 3))
+    events[1] = query(3)
+    events[2] = side((2, 3)) + query(1)
+    events[3] = side((1, 1), (0, 1), (2, 1)) + query(2) + side((3, 1))
+    events[5] = side((1, 3), (3, 3))
+    events[9] = side((1, 2), (2, 2), (0, 2), (3, 2))
     last_of = {q: max(n for n, s in enumerate(STEPS) if s[0] == q) for q in range(nx)}
     first_of = {dy: min(n for n, s in enumerate(STEPS) if s[1] == dy) for dy in range(ny)}
 

time: 30.3 us -> 30.6 us (level)
  no operation moved by 1% of the time
where the time goes in v12:
time: 30.6 us
  Pallas kernels  29.8 us (97%)
  local copies, waits for them, and re-layouts  0.75 us (2%)
    pallas_call x1, Pallas kernels, local_layer(): pl.pallas_call(functools.partial(kernel, dims), out_shape=jax.ShapeDtypeS...  29.8 us
    unnamed x1, local copies, waits for them, and re-layouts  0.75 us

profile of v12, /device:TPU:97, one launch (start us, length us, event | category | flops | bytes accessed | tf_op | source)
XLA Modules:
  0.0 30.6 jit_solution(17914385546883119971)
XLA Ops:
  0.0 29.8 %shard_map.37 = bf16[96,2048]{1,0:T(8,128)(2,1)S(1)} custom-call(bf16[96,2048]{1,0:T(8,128)(2,1)} %bitcast.9, bf16[3072,2048]{1,0:T(8,128)(2,1)} %bitcast.7, bf16[2048,2048]{1,0:T(8,128)(2,1)} %bitcast.8), custom_call_target="tpu_custom_call" | custom-call | tf_op jit(solution)/shard_map/pallas_call | solution.py:295
  29.8 0.7 %copy.5 = bf16[1,96,2048]{2,1,0:T(8,128)(2,1)} copy(bf16[1,96,2048]{2,1,0:T(8,128)(2,1)S(1)} %bitcast.6) | data formatting | bytes 786432

commit v13 on v11

--- a/solution.py
+++ b/solution.py
@@ -130,8 +130,15 @@
             else:
                 spread(src, lambda dy: kv_half(0, dy, 0), 0)
                 kv_buf[kv_at(0, 0):kv_at(0, 0) + dev_tokens] = kv_all[2 * i + k]
-    o_load = pltpu.make_async_copy(wout_hbm, w_o, load_sem.at[1 + 5 * nx])
-    o_load.start()
+    o_loads = []
+    for i, dx in enumerate(O_ORDER):
+        for r in range(2):
+            src = ((core if r == 0 else other) * kv_local + head_at(dx)) * q_rows
+            copy = pltpu.make_async_copy(
+                wout_hbm.at[pl.ds(pl.multiple_of(src, q_rows), q_rows)],
+                w_o.at[pl.ds((2 * i + r) * q_rows, q_rows)], load_sem.at[1 + 5 * nx + 2 * i + r])
+            copy.start()
+            o_loads.append(copy)
 
     x_copy.wait()
     x_ext[chip_tokens:chip_tokens + tail] = x_ext[main:chip_tokens]
@@ -254,19 +261,18 @@
         if ends:
             finish(STEPS[n - 1][0])
 
-    o_load.wait()
+    for copy in o_loads:
+        copy.wait()
     for i, dx in enumerate(O_ORDER):
         if i == nx - 1:
             for ref, sem in ((kv_buf.at[pl.ds(0, (nx * ny - 1) * chip_tokens)], kv_send.at[0]), (kv_all.at[0], kv_send.at[1]), (q_all.at[pl.ds(0, nx - 1)], q_send), (o_all.at[:, pl.ds(0, nx - 1)], o_send_sem.at[0]), (o_all.at[1, 0], o_send_sem.at[1])):
                 remote(ref, ref, sem, x_sem.at[1], partner).wait_send()
-        total = None
         for r in range(2):
             if dx or r:
                 arrive(o_all.at[r, dx], o_recv.at[r, dx])
-            first = ((core if r == 0 else other) * kv_local + head_at(dx)) * q_rows
-            term = jnp.dot(o_all[r, dx], w_o[pl.ds(pl.multiple_of(first, q_rows), q_rows)],
-                           preferred_element_type=jnp.float32)
-            total = term if total is None else total + term
+        total = jnp.dot(
+            jnp.concatenate([o_all[0, dx], o_all[1, dx]], axis=1), w_o[2 * i * q_rows:(2 * i + 2) * q_rows],
+            preferred_element_type=jnp.float32)
         if i == 0:
             y_acc[...] = total
         elif i < nx - 1:
@@ -316,7 +322,7 @@
                 pltpu.VMEM((nx, 2 * tokens, q_rows), half),
                 pltpu.VMEM((2, nx, tokens, q_rows), half),
                 pltpu.VMEM((tokens, width), jnp.float32),
-                pltpu.SemaphoreType.DMA((2 + 5 * nx,)),
+                pltpu.SemaphoreType.DMA((1 + 7 * nx,)),
                 pltpu.SemaphoreType.DMA((2,)),
                 pltpu.SemaphoreType.DMA((2,)),
                 pltpu.SemaphoreType.DMA((ny, nx)),

time: 30.3 us -> 30.3 us (level)
  no operation moved by 1% of the time
where the time goes in v13:
time: 30.3 us
  Pallas kernels  29.5 us (97%)
  local copies, waits for them, and re-layouts  0.75 us (2%)
    pallas_call x1, Pallas kernels, local_layer(): pl.pallas_call(functools.partial(kernel, dims), out_shape=jax.ShapeDtypeS...  29.5 us
    unnamed x1, local copies, waits for them, and re-layouts  0.75 us

profile of v13, /device:TPU:97, one launch (start us, length us, event | category | flops | bytes accessed | tf_op | source)
XLA Modules:
  0.0 30.3 jit_solution(6411527499056989253)
XLA Ops:
  0.0 29.5 %shard_map.37 = bf16[96,2048]{1,0:T(8,128)(2,1)S(1)} custom-call(bf16[96,2048]{1,0:T(8,128)(2,1)} %bitcast.9, bf16[3072,2048]{1,0:T(8,128)(2,1)} %bitcast.7, bf16[2048,2048]{1,0:T(8,128)(2,1)} %bitcast.8), custom_call_target="tpu_custom_call" | custom-call | tf_op jit(solution)/shard_map/pallas_call | solution.py:301
  29.5 0.7 %copy.5 = bf16[1,96,2048]{2,1,0:T(8,128)(2,1)} copy(bf16[1,96,2048]{2,1,0:T(8,128)(2,1)S(1)} %bitcast.6) | data formatting | bytes 786432

commit v14 on v13

--- a/solution.py
+++ b/solution.py
@@ -15,7 +15,7 @@
 
 STEPS = (
     (0, 0), (1, 0), (3, 0), (1, 1), (2, 3), (2, 0), (1, 3), (2, 1),
-    (2, 2), (3, 2), (1, 2), (3, 3), (3, 1), (0, 3), (0, 1), (0, 2),
+    (2, 2), (1, 2), (3, 2), (3, 3), (3, 1), (0, 3), (0, 1), (0, 2),
 )
 SLOTS = (("s", 0), ("a", 0), ("s", 1), ("a", 1), ("s", 2), ("a", 2))
 END_SLOTS = (("s", 0), ("a", 0), ("a", 1), ("s", 1), ("a", 2), ("s", 2))

time: 30.3 us -> 30.5 us (level)
  no operation moved by 1% of the time
where the time goes in v14:
time: 30.5 us; the launch traced here: 30.4 us
  Pallas kernels  29.6 us (97%)
  local copies, waits for them, and re-layouts  0.75 us (2%)
    pallas_call x1, Pallas kernels, local_layer(): pl.pallas_call(functools.partial(kernel, dims), out_shape=jax.ShapeDtypeS...  29.6 us
    unnamed x1, local copies, waits for them, and re-layouts  0.75 us

profile of v14, /device:TPU:97, one launch (start us, length us, event | category | flops | bytes accessed | tf_op | source)
XLA Modules:
  0.0 30.4 jit_solution(9905441581173414344)
XLA Ops:
  0.0 29.6 %shard_map.37 = bf16[96,2048]{1,0:T(8,128)(2,1)S(1)} custom-call(bf16[96,2048]{1,0:T(8,128)(2,1)} %bitcast.9, bf16[3072,2048]{1,0:T(8,128)(2,1)} %bitcast.7, bf16[2048,2048]{1,0:T(8,128)(2,1)} %bitcast.8), custom_call_target="tpu_custom_call" | custom-call | tf_op jit(solution)/shard_map/pallas_call | solution.py:301
  29.6 0.7 %copy.5 = bf16[1,96,2048]{2,1,0:T(8,128)(2,1)} copy(bf16[1,96,2048]{2,1,0:T(8,128)(2,1)S(1)} %bitcast.6) | data formatting | bytes 786432

commit v15 on v13

--- a/solution.py
+++ b/solution.py
@@ -94,9 +94,6 @@
     x_copy = remote(x_ext.at[own_rows], x_ext.at[own_rows], x_sem.at[0], x_sem.at[1], partner)
     x_copy.start()
     q_t[:, head_dim:, :] = jnp.zeros((nx, LANES - head_dim, rows), jnp.bfloat16)
-    acc[...] = jnp.zeros_like(acc)
-    m_run[...] = jnp.full_like(m_run, -jnp.inf)
-    l_run[...] = jnp.zeros_like(l_run)
 
     def kv_at(dx, dy):
         return dy * row_keys + dx * chip_tokens
@@ -189,23 +186,32 @@
     def keys(dy):
         return kv_buf[kv_at(0, dy):kv_at(0, dy) + row_keys]
 
+    def first_step(n):
+        return all(step[0] != STEPS[n][0] for step in STEPS[:n])
+
     def score(n, q, dy, t):
         cols = slice(t * TILE, (t + 1) * TILE)
         scores = jnp.dot(keys(dy), q_t[q, :, cols], preferred_element_type=jnp.float32)
-        old_max = m_run[q, :, cols]
-        new_max = jnp.maximum(old_max, jnp.max(scores, axis=0, keepdims=True))
+        new_max = jnp.max(scores, axis=0, keepdims=True)
+        if not first_step(n):
+            old_max = m_run[q, :, cols]
+            new_max = jnp.maximum(old_max, new_max)
+            r_cur[n % 2, :, cols] = jnp.exp2((old_max - new_max) * scale)
         m_run[q, :, cols] = new_max
         m_cur[n % 2, :, cols] = new_max
-        r_cur[n % 2, :, cols] = jnp.exp2((old_max - new_max) * scale)
         s_buf[n % 2, t] = scores
 
     def absorb(n, q, dy, t):
         cols = slice(t * TILE, (t + 1) * TILE)
-        rescale = r_cur[n % 2, :, cols]
         weights = jnp.exp2((s_buf[n % 2, t] - m_cur[n % 2, :, cols]) * scale)
-        l_run[q, :, cols] = l_run[q, :, cols] * rescale + jnp.sum(weights, axis=0, keepdims=True)
-        acc[q, :, cols] = acc[q, :, cols] * rescale + jnp.dot(
-            v_t[dy], weights.astype(jnp.bfloat16), preferred_element_type=jnp.float32)
+        sums = jnp.sum(weights, axis=0, keepdims=True)
+        out = jnp.dot(v_t[dy], weights.astype(jnp.bfloat16), preferred_element_type=jnp.float32)
+        if not first_step(n):
+            rescale = r_cur[n % 2, :, cols]
+            sums = l_run[q, :, cols] * rescale + sums
+            out = acc[q, :, cols] * rescale + out
+        l_run[q, :, cols] = sums
+        acc[q, :, cols] = out
 
     def finish(q):
         out = acc[q] / l_run[q]

time: 30.3 us -> 30.3 us (level)
  no operation moved by 1% of the time
where the time goes in v15:
time: 30.3 us; the launch traced here: 30.2 us
  Pallas kernels  29.4 us (97%)
  local copies, waits for them, and re-layouts  0.75 us (2%)
    pallas_call x1, Pallas kernels, local_layer(): pl.pallas_call(functools.partial(kernel, dims), out_shape=jax.ShapeDtypeS...  29.4 us
    unnamed x1, local copies, waits for them, and re-layouts  0.75 us

profile of v15, /device:TPU:97, one launch (start us, length us, event | category | flops | bytes accessed | tf_op | source)
XLA Modules:
  0.0 30.2 jit_solution(10633915528772331263)
XLA Ops:
  0.0 29.4 %shard_map.37 = bf16[96,2048]{1,0:T(8,128)(2,1)S(1)} custom-call(bf16[96,2048]{1,0:T(8,128)(2,1)} %bitcast.9, bf16[3072,2048]{1,0:T(8,128)(2,1)} %bitcast.7, bf16[2048,2048]{1,0:T(8,128)(2,1)} %bitcast.8), custom_call_target="tpu_custom_call" | custom-call | tf_op jit(solution)/shard_map/pallas_call | solution.py:307
  29.4 0.7 %copy.5 = bf16[1,96,2048]{2,1,0:T(8,128)(2,1)} copy(bf16[1,96,2048]{2,1,0:T(8,128)(2,1)S(1)} %bitcast.6) | data formatting | bytes 786432
